TPU v7x, 256 devices: a whole 4x4x8 slice. The times are simulated.
256 devices in a mesh: gx: 8 (over z_lo, core), gy: 32 (over y, x, z_hi).
Axes of the slice: x: 4, y: 4, z: 8 (z_hi: 2, z_lo: 4; z = z_hi * 4 + z_lo), core: 2. Of those that a mesh axis runs over, the one named last changes fastest.
Arguments:
- echoes: bfloat16 [128, 512, 16, 200], P('gx', 'gy'), may hold values from -6 to 6
- start: float32 [200, 32], replicated, may hold values from -6 to 6
- ranks: int32 [8, 32, 1], P('gx', 'gy'), may hold values from 2 to 32
- counts: int32 [8, 32, 1], P('gx', 'gy'), may hold values from 1 to 4
Outputs:
- filtered: bfloat16 [128, 512, 16, 200], P('gx', 'gy')
All inputs are finite; a program needn't handle non-finite values.
Results may differ from a plain program's by a relative error of at most 0.0075.
Values may be sent and summed in bfloat16 or wider, within the bound.
No kernel may reach another device: no remote copies, remote signals or barrier semaphores. Data moves between devices by JAX's collectives and lax.ppermute only.
A program may use at most 128 MiB of HBM per device.

v0:
```python
import jax
import jax.numpy as jnp
from jax import lax
from jax.sharding import PartitionSpec as P

BZ = 16
K = 32
ITERS = 4


def passed_along(block, axis, distance):
    devices = range(lax.axis_size(axis))
    route = [(i - distance, i) for i in devices if i - distance in devices]
    return lax.ppermute(block, axis, route)


def tent(offset, span):
    inside = (offset >= 0.0) & (offset < span)
    return jnp.where(inside, 1.0 + jnp.minimum(offset, span - 1.0 - offset), 0.0)


def segment_grams(region):
    sizex, sizey, depth, frames = region.shape
    half = BZ // 2
    parts = region.reshape(sizex, sizey, depth // half, half, frames)
    return jnp.einsum("xyshf,xyshg->sfg", parts, parts, preferred_element_type=jnp.float32)


def subspace(grams, start, counts):
    basis = jnp.broadcast_to(start, (grams.shape[0],) + start.shape)
    for turn in range(ITERS):
        moved = jnp.einsum("sfg,sgk->sfk", grams, basis, precision=lax.Precision.HIGHEST)
        inner = jnp.einsum("sfk,sfl->skl", moved, moved, precision=lax.Precision.HIGHEST)
        factor = jnp.linalg.cholesky(inner)
        solved = lax.linalg.triangular_solve(
            factor, moved, left_side=False, lower=True, transpose_a=True
        )
        basis = jnp.where((turn < counts)[:, None, None], solved, basis)
    return basis


def truncated_bases(grams, ranks, counts, start):
    basis = subspace(grams, start, counts)
    keep = (jnp.arange(K)[None, :] < ranks[:, None]).astype(jnp.float32)
    return (basis * keep[:, None, :]).astype(jnp.bfloat16)


def project_quarter(local, vectors_all, start_x, start_y):
    span_x, span_y, depth, frames = local.shape
    weight = (
        tent(jnp.arange(span_x, dtype=jnp.float32) + start_x, float(2 * span_x))[
            :, None, None, None
        ]
        * tent(jnp.arange(span_y, dtype=jnp.float32) + start_y, float(2 * span_y))[
            None, :, None, None
        ]
        * tent(jnp.arange(BZ, dtype=jnp.float32), float(BZ))[None, None, :, None]
    )

    def add_block(index, total):
        vectors = vectors_all[index]
        coeff = jnp.einsum(
            "xyzf,fk->xyzk", local, vectors, preferred_element_type=jnp.float32
        ).astype(jnp.bfloat16)
        clutter = jnp.einsum("xyzk,fk->xyzf", coeff, vectors, preferred_element_type=jnp.float32)
        contrib = weight * (local.astype(jnp.float32) - clutter)
        return total + contrib

    return lax.fori_loop(0, vectors_all.shape[0], add_block, jnp.zeros(local.shape, jnp.float32))


def body(echoes, start, ranks, counts):
    span, _, depth, frames = echoes.shape
    row = lax.axis_index("gx")
    col = lax.axis_index("gy")
    rows = lax.axis_size("gx")
    cols = lax.axis_size("gy")
    nblocks = 2 * depth // BZ - 1
    pieces = segment_grams(echoes)
    from_right = passed_along(pieces.astype(jnp.bfloat16), "gy", -1).astype(pieces.dtype)
    upper = pieces + from_right
    from_below = passed_along(upper.astype(jnp.bfloat16), "gx", -1).astype(upper.dtype)
    segments = upper + from_below
    grams = (segments[:-1] + segments[1:]) / float(4 * span * span * BZ)
    own_vectors = truncated_bases(grams, ranks[0, 0], counts[0, 0], start)
    left_vectors = passed_along(own_vectors, "gy", 1)
    paired = jnp.stack([own_vectors, left_vectors], 0)
    above = passed_along(paired, "gx", 1)
    last_row = row <= rows - 2
    first_row = row >= 1
    last_col = col <= cols - 2
    first_col = col >= 1
    total = jnp.where(last_row & last_col, project_quarter(echoes, own_vectors, 0.0, 0.0), 0.0)
    total = total + jnp.where(
        last_row & first_col, project_quarter(echoes, left_vectors, 0.0, float(span)), 0.0
    )
    total = total + jnp.where(
        first_row & last_col, project_quarter(echoes, above[0], float(span), 0.0), 0.0
    )
    total = total + jnp.where(
        first_row & first_col, project_quarter(echoes, above[1], float(span), float(span)), 0.0
    )
    width = float(2 * span)
    local = jnp.arange(span, dtype=jnp.float32)
    coverx = tent(local, width) * (row <= rows - 2).astype(jnp.float32) + tent(
        local + span, width
    ) * (row >= 1).astype(jnp.float32)
    covery = tent(local, width) * (col <= cols - 2).astype(jnp.float32) + tent(
        local + span, width
    ) * (col >= 1).astype(jnp.float32)
    posz = jnp.arange(depth, dtype=jnp.float32)
    coverz = jnp.sum(
        tent(posz[None, :] - BZ // 2 * jnp.arange(nblocks, dtype=jnp.float32)[:, None], float(BZ)),
        axis=0,
    )
    cover = coverx[:, None, None, None] * covery[None, :, None, None] * coverz[None, None, :, None]
    return (total / cover).astype(jnp.bfloat16)


def solution(mesh):
    placed = (P("gx", "gy", None, None), P(), P("gx", "gy", None), P("gx", "gy", None))
    return jax.shard_map(
        body, mesh=mesh, in_specs=placed, out_specs=P("gx", "gy", None, None), check_vma=False
    )
```

profile of v0, /device:TPU:49, one launch (start us, length us, event | category | flops | bytes accessed | tf_op | source)
XLA Modules:
  0.0 87.3 jit_solution(7967920143017670596)
XLA Ops:
  0.0 3.1 %fusion.65 = (bf16[2,200,200]{2,1,0:T(8,128)(2,1)S(1)}, f32[2,200,200]{2,1,0:T(8,128)S(1)}) fusion(bf16[16,16,16,200]{3,2,1,0:T(8,128)(2,1)} %param.7), kind=kOutput, calls=%fused_computation.115 | convolution fusion | flops 327760000 | bytes 2118400 | tf_op jit(solution)/shard_map/xyshf,xyshg->sfg/dot_general | solution.py:26
  3.1 10.1 %collective-permute-start = (bf16[2,200,200]{2,1,0:T(8,128)(2,1)S(1)}, bf16[2,200,200]{2,1,0:T(8,128)(2,1)S(1)}, u32[]{:S(2)}, u32[]{:S(2)}) collective-permute-start(bf16[2,200,200]{2,1,0:T(8,128)(2,1)S(1)} %get-tuple-element.74), channel_id=1, source_target_pairs={{1,0},{2,1},{3,2},{4,3},{5,4},{6,5},{7,6},{8,7},{9,8},{10,9},{11,1... | collective-permute-start | bytes 480008 | tf_op jit(solution)/shard_map/ppermute | solution.py:14
  13.5 7.0 %collective-permute-done = bf16[2,200,200]{2,1,0:T(8,128)(2,1)S(1)} collective-permute-done((bf16[2,200,200]{2,1,0:T(8,128)(2,1)S(1)}, bf16[2,200,200]{2,1,0:T(8,128)(2,1)S(1)}, u32[]{:S(2)}, u32[]{:S(2)}) %collective-permute-start) | collective-permute-done | bytes 160032 | tf_op jit(solution)/shard_map/ppermute | solution.py:14
  20.6 4.3 %collective-permute-start.1 = (bf16[2,200,200]{2,1,0:T(8,128)(2,1)S(1)}, bf16[2,200,200]{2,1,0:T(8,128)(2,1)S(1)}, u32[]{:S(2)}, u32[]{:S(2)}) collective-permute-start(bf16[2,200,200]{2,1,0:T(8,128)(2,1)S(1)} %fusion.31), channel_id=1, source_target_pairs={{32,0},{64,32},{96,64},{128,96},{160,128},{192,160},{224,192},{33,... | collective-permute-start | bytes 480008 | tf_op jit(solution)/shard_map/ppermute | solution.py:14
  24.9 0.9 %broadcast_multiply_fusion.4 = (f32[16,16,16]{2,1,0:T(8,128)S(1)}, f32[16,16,16]{2,1,0:T(8,128)S(1)}, f32[16,16,16]{2,1,0:T(8,128)S(1)}, f32[16,16,16]{2,1,0:T(8,128)}, f32[16,16,16]{2,1,0:T(8,128)}) fusion(f32[16]{0:T(128)S(1)} %compare_select_fusion, f32[16,16]{1,0:T(8,128)S(1)} %get-tuple-element.72, f32[16,16]{1,0:T(8,128)S(1)} %get-tuple-element.53, ...), kind=kLoop, calls=%fused_computation.51 | loop fusion | flops 20480 | bytes 87104 | tf_op jit(solution)/shard_map/mul | solution.py:51
  27.1 0.9 %collective-permute-done.1 = bf16[2,200,200]{2,1,0:T(8,128)(2,1)S(1)} collective-permute-done((bf16[2,200,200]{2,1,0:T(8,128)(2,1)S(1)}, bf16[2,200,200]{2,1,0:T(8,128)(2,1)S(1)}, u32[]{:S(2)}, u32[]{:S(2)}) %collective-permute-start.1) | collective-permute-done | bytes 160032 | tf_op jit(solution)/shard_map/ppermute | solution.py:14
  28.7 2.9 %custom-call.12 = f32[1,32,32]{2,1,0:T(8,128)S(1)} custom-call(f32[1,32,32]{2,1,0:T(8,128)S(1)} %fusion.51), custom_call_target="Cholesky" | custom-call | tf_op jit(solution)/shard_map/jit(cholesky)/cholesky | solution.py:34
  31.6 0.7 compare_reduce_fusion.3
  32.9 2.4 %custom-call.13 = f32[1,1,32,32]{2,3,1,0:T(8,128)S(1)} custom-call(f32[1,1,32,32]{3,2,1,0:T(8,128)S(1)} %fusion.40), custom_call_target="InvertDiagBlocksLowerTriangular" | custom-call | tf_op jit(solution)/shard_map/triangular_solve/custom-call.0 | solution.py:35
  36.2 2.9 %custom-call.14 = f32[1,32,32]{2,1,0:T(8,128)S(1)} custom-call(f32[1,32,32]{2,1,0:T(8,128)S(1)} %fusion.50), custom_call_target="Cholesky" | custom-call | tf_op jit(solution)/shard_map/jit(cholesky)/cholesky | solution.py:34
  39.1 0.7 compare_reduce_fusion.2
  40.5 2.4 %custom-call.15 = f32[1,1,32,32]{2,3,1,0:T(8,128)S(1)} custom-call(f32[1,1,32,32]{3,2,1,0:T(8,128)S(1)} %fusion.41), custom_call_target="InvertDiagBlocksLowerTriangular" | custom-call | tf_op jit(solution)/shard_map/triangular_solve/custom-call.0 | solution.py:35
  43.7 2.9 %custom-call.16 = f32[1,32,32]{2,1,0:T(8,128)S(1)} custom-call(f32[1,32,32]{2,1,0:T(8,128)S(1)} %fusion.49), custom_call_target="Cholesky" | custom-call | tf_op jit(solution)/shard_map/jit(cholesky)/cholesky | solution.py:34
  46.7 0.7 compare_reduce_fusion.1
  48.0 2.4 %custom-call.17 = f32[1,1,32,32]{2,3,1,0:T(8,128)S(1)} custom-call(f32[1,1,32,32]{3,2,1,0:T(8,128)S(1)} %fusion.42), custom_call_target="InvertDiagBlocksLowerTriangular" | custom-call | tf_op jit(solution)/shard_map/triangular_solve/custom-call.0 | solution.py:35
  51.3 2.9 %custom-call.18 = f32[1,32,32]{2,1,0:T(8,128)S(1)} custom-call(f32[1,32,32]{2,1,0:T(8,128)S(1)} %fusion.48), custom_call_target="Cholesky" | custom-call | tf_op jit(solution)/shard_map/jit(cholesky)/cholesky | solution.py:34
  55.4 2.4 %custom-call.19 = f32[1,1,32,32]{2,3,1,0:T(8,128)S(1)} custom-call(f32[1,1,32,32]{3,2,1,0:T(8,128)S(1)} %fusion.43), custom_call_target="InvertDiagBlocksLowerTriangular" | custom-call | tf_op jit(solution)/shard_map/triangular_solve/custom-call.0 | solution.py:35
  58.1 7.6 %collective-permute-start.2 = (bf16[1,200,32]{1,2,0:T(8,128)(2,1)S(1)}, bf16[1,200,32]{1,2,0:T(8,128)(2,1)S(1)}, u32[]{:S(2)}, u32[]{:S(2)}) collective-permute-start(bf16[1,200,32]{1,2,0:T(8,128)(2,1)S(1)} %fusion.30), channel_id=1, source_target_pairs={{0,1},{1,2},{2,3},{3,4},{4,5},{5,6},{6,7},{7,8},{8,9},{9,10},{10,1... | collective-permute-start | bytes 38408 | tf_op jit(solution)/shard_map/ppermute | solution.py:14
  65.8 3.3 %fusion.16 = f32[16,16,16,200]{3,2,1,0:T(8,128)} fusion(bf16[16,16,16,200]{3,2,1,0:T(8,128)(2,1)S(1)} %copy-done, bf16[1,200,32]{1,2,0:T(8,128)(2,1)S(1)} %fusion.30), kind=kOutput, calls=%fused_computation.24 | convolution fusion | flops 104988672 | bytes 4928000 | tf_op jit(solution)/shard_map/while/body/eval_jaxpr/xyzk,fk->xyzf/dot_general | solution.py:65
  69.1 1.8 %collective-permute-done.2 = bf16[1,200,32]{1,2,0:T(8,128)(2,1)S(1)} collective-permute-done((bf16[1,200,32]{1,2,0:T(8,128)(2,1)S(1)}, bf16[1,200,32]{1,2,0:T(8,128)(2,1)S(1)}, u32[]{:S(2)}, u32[]{:S(2)}) %collective-permute-start.2) | collective-permute-done | bytes 12832 | tf_op jit(solution)/shard_map/ppermute | solution.py:14
  70.9 2.6 %collective-permute-start.3 = (bf16[2,1,200,32]{2,3,1,0:T(8,128)(2,1)S(1)}, bf16[2,1,200,32]{2,3,1,0:T(8,128)(2,1)S(1)}, u32[]{:S(2)}, u32[]{:S(2)}) collective-permute-start(bf16[2,1,200,32]{2,3,1,0:T(8,128)(2,1)S(1)} %pad_maximum_fusion), channel_id=1, source_target_pairs={{0,32},{32,64},{64,96},{96,128},{128,160},{160,192},{192,224},{1,3... | collective-permute-start | bytes 76808 | tf_op jit(solution)/shard_map/ppermute | solution.py:14
  73.6 3.3 %fusion.18 = f32[16,16,16,200]{3,2,1,0:T(8,128)} fusion(bf16[16,16,16,200]{3,2,1,0:T(8,128)(2,1)S(1)} %copy-done, bf16[1,200,32]{1,2,0:T(8,128)(2,1)S(1)} %collective-permute-done.2), kind=kOutput, calls=%fused_computation.26 | convolution fusion | flops 104988672 | bytes 4928000 | tf_op jit(solution)/shard_map/while/body/eval_jaxpr/xyzk,fk->xyzf/dot_general | solution.py:65
  76.9 3.3 %fusion.20 = f32[16,16,16,200]{3,2,1,0:T(8,128)} fusion(bf16[16,16,16,200]{3,2,1,0:T(8,128)(2,1)S(1)} %copy-done, bf16[2,1,200,32]{2,3,1,0:T(8,128)(2,1)S(1)} %collective-permute-done.3), kind=kOutput, calls=%fused_computation.28 | convolution fusion | flops 104988672 | bytes 4940800 | tf_op jit(solution)/shard_map/while/body/eval_jaxpr/xyzk,fk->xyzf/dot_general | solution.py:65
  80.1 7.2 %fusion.12 = bf16[16,16,16,200]{3,2,1,0:T(8,128)(2,1)} fusion(f32[16,16,16,200]{3,2,1,0:T(8,128)} %fusion.20, f32[16,16,16,200]{3,2,1,0:T(8,128)} %fusion.18, f32[16,16,16,200]{3,2,1,0:T(8,128)} %fusion.16, bf16[16,16,16,200]{3,2,1,0:T(8,128)(2,1)S(1)} %copy-done, f32[16,16,16]{2,1,0:T(8,128)S(1)} %copy-done.3, f32[16,16,16]{2,1,0:T(8,128)S(1)} %copy-done.2, ...), kind=kOutput, calls=%fused_computation.16 | convolution fusion | flops 119734272 | bytes 16351236 | tf_op jit(solution)/shard_map/while/body/eval_jaxpr/xyzk,fk->xyzf/dot_general | solution.py:65
  (48 shorter events, 6.8 us)
Async XLA Ops:
  0.0 28.1 %copy-start.1 = (f32[200,32]{0,1:T(8,128)S(1)}, f32[200,32]{0,1:T(8,128)}, u32[]{:S(2)}) copy-start(f32[200,32]{0,1:T(8,128)} %param.8) | copy-start | bytes 76804
  3.1 62.7 %copy-start = (bf16[16,16,16,200]{3,2,1,0:T(8,128)(2,1)S(1)}, bf16[16,16,16,200]{3,2,1,0:T(8,128)(2,1)}, u32[]{:S(2)}) copy-start(bf16[16,16,16,200]{3,2,1,0:T(8,128)(2,1)} %param.7) | copy-start | bytes 4915204
  3.1 17.4 %collective-permute-start = (bf16[2,200,200]{2,1,0:T(8,128)(2,1)S(1)}, bf16[2,200,200]{2,1,0:T(8,128)(2,1)S(1)}, u32[]{:S(2)}, u32[]{:S(2)}) collective-permute-start(bf16[2,200,200]{2,1,0:T(8,128)(2,1)S(1)} %get-tuple-element.74), channel_id=1, source_target_pairs={{1,0},{2,1},{3,2},{4,3},{5,4},{6,5},{7,6},{8,7},{9,8},{10,9},{11,1... | collective-permute-start | bytes 480008 | tf_op jit(solution)/shard_map/ppermute | solution.py:14
  20.6 7.4 %collective-permute-start.1 = (bf16[2,200,200]{2,1,0:T(8,128)(2,1)S(1)}, bf16[2,200,200]{2,1,0:T(8,128)(2,1)S(1)}, u32[]{:S(2)}, u32[]{:S(2)}) collective-permute-start(bf16[2,200,200]{2,1,0:T(8,128)(2,1)S(1)} %fusion.31), channel_id=1, source_target_pairs={{32,0},{64,32},{96,64},{128,96},{160,128},{192,160},{224,192},{33,... | collective-permute-start | bytes 480008 | tf_op jit(solution)/shard_map/ppermute | solution.py:14
  58.1 12.8 %collective-permute-start.2 = (bf16[1,200,32]{1,2,0:T(8,128)(2,1)S(1)}, bf16[1,200,32]{1,2,0:T(8,128)(2,1)S(1)}, u32[]{:S(2)}, u32[]{:S(2)}) collective-permute-start(bf16[1,200,32]{1,2,0:T(8,128)(2,1)S(1)} %fusion.30), channel_id=1, source_target_pairs={{0,1},{1,2},{2,3},{3,4},{4,5},{5,6},{6,7},{7,8},{8,9},{9,10},{10,1... | collective-permute-start | bytes 38408 | tf_op jit(solution)/shard_map/ppermute | solution.py:14
  70.9 5.9 %collective-permute-start.3 = (bf16[2,1,200,32]{2,3,1,0:T(8,128)(2,1)S(1)}, bf16[2,1,200,32]{2,3,1,0:T(8,128)(2,1)S(1)}, u32[]{:S(2)}, u32[]{:S(2)}) collective-permute-start(bf16[2,1,200,32]{2,3,1,0:T(8,128)(2,1)S(1)} %pad_maximum_fusion), channel_id=1, source_target_pairs={{0,32},{32,64},{64,96},{96,128},{128,160},{160,192},{192,224},{1,3... | collective-permute-start | bytes 76808 | tf_op jit(solution)/shard_map/ppermute | solution.py:14
  76.9 3.3 %copy-start.2 = (f32[16,16,16]{2,1,0:T(8,128)S(1)}, f32[16,16,16]{2,1,0:T(8,128)}, u32[]{:S(2)}) copy-start(f32[16,16,16]{2,1,0:T(8,128)} %get-tuple-element.64) | copy-start | bytes 49156
  76.9 3.3 %copy-start.3 = (f32[16,16,16]{2,1,0:T(8,128)S(1)}, f32[16,16,16]{2,1,0:T(8,128)}, u32[]{:S(2)}) copy-start(f32[16,16,16]{2,1,0:T(8,128)} %get-tuple-element.65) | copy-start | bytes 49156
where the time goes:
time: 89 us; the launch traced here: 87.3 us
  other arithmetic  28 us (31%)
  starting transfers between devices  24.7 us (28%)
  matrix products  23 us (26%)
  waiting for transfers between devices  9.75 us (11%)
  between operations  1.57 us (2%)
    ppermute x4, starting transfers between devices, passed_along(): return lax.ppermute(block, axis, route)  24.7 us
    dot_general x4, matrix products, add_block(): jnp.einsum('xyzk,fk->xyzf', coeff, vectors, preferred_element_type=jnp.fl...  17.1 us
    another operation x12, other arithmetic, subspace(): factor = jnp.linalg.cholesky(inner)  14.5 us
    another operation x8, other arithmetic, subspace(): lax.linalg.triangular_solve(factor, moved, left_side=False, lower=True, t...  12.2 us
    ppermute x4, waiting for transfers between devices, passed_along(): return lax.ppermute(block, axis, route)  9.75 us
    dot_general x1, matrix products, segment_grams(): jnp.einsum('xyshf,xyshg->sfg', parts, parts, preferred_element_type=jnp.f...  3.1 us
  transfers between devices with their start and end apart: 4, of which 3 were waited for; matrix products, arithmetic and copies ran while one was open for 9% of the time, Pallas kernels for 0%

commit v1 on v0

v1 whole, which is shorter than its diff:
```python
import functools

import jax
import jax.numpy as jnp
from jax import lax
from jax.experimental import pallas as pl
from jax.experimental.pallas import tpu as pltpu
from jax.sharding import PartitionSpec as P

BZ = 16
K = 32
ITERS = 4
LANES = 128
META = 8
GRAM_CHUNK = 1024
PROJ_CHUNK = 512
PANEL = 16

f32 = jnp.float32
bf16 = jnp.bfloat16


def iota(shape, dim):
    return lax.broadcasted_iota(jnp.int32, shape, dim)


def gram_kernel(rank_ref, count_ref, c_ref, own_ref, sent_ref, acc_ref):
    step = pl.program_id(0)
    frames = acc_ref.shape[0]
    c = c_ref[...]
    part = lax.dot_general(c, c, (((0,), (0,)), ((), ())), preferred_element_type=f32)

    @pl.when(step == 0)
    def _():
        acc_ref[...] = part

    @pl.when(step > 0)
    def _():
        acc_ref[...] += part

    @pl.when(step == pl.num_programs(0) - 1)
    def _():
        rest = frames - LANES
        first = LANES - rest
        own_ref[...] = acc_ref[:, :LANES]
        shape = (rest, rest)
        low = iota(shape, 1) <= iota(shape, 0)
        own_ref[first:LANES, :rest] = jnp.where(
            low, acc_ref[LANES:, LANES:], acc_ref[first:LANES, :rest]
        )
        tile = own_ref[META : META + 8, :]
        row, lane = iota(tile.shape, 0), iota(tile.shape, 1)
        rank = rank_ref[0].astype(f32)
        count = count_ref[0].astype(f32)
        tile = jnp.where((row == 0) & (lane == 0), rank, tile)
        tile = jnp.where((row == 0) & (lane == 1), count, tile)
        own_ref[META : META + 8, :] = tile
        sent_ref[...] = own_ref[...].astype(bf16)


def own_gram(voxels, rank, count):
    m, frames = voxels.shape
    steps = m // GRAM_CHUNK
    return pl.pallas_call(
        gram_kernel,
        grid=(steps,),
        in_specs=[
            pl.BlockSpec(memory_space=pltpu.SMEM),
            pl.BlockSpec(memory_space=pltpu.SMEM),
            pl.BlockSpec((GRAM_CHUNK, frames), lambda i: (i, 0)),
        ],
        out_specs=[
            pl.BlockSpec((frames, LANES), lambda i: (0, 0)),
            pl.BlockSpec((frames, LANES), lambda i: (0, 0)),
        ],
        out_shape=[
            jax.ShapeDtypeStruct((frames, LANES), f32),
            jax.ShapeDtypeStruct((frames, LANES), bf16),
        ],
        scratch_shapes=[pltpu.VMEM((frames, frames), f32)],
        compiler_params=pltpu.CompilerParams(dimension_semantics=("arbitrary",)),
        cost_estimate=pl.CostEstimate(
            flops=2 * m * frames * frames, bytes_accessed=2 * m * frames, transcendentals=0
        ),
        name="own_gram",
    )(rank, count, voxels)


def split(x):
    high = x.astype(bf16)
    low = (x - high.astype(f32)).astype(bf16)
    return high, low


def unpacked(pk):
    frames = pk.shape[0]
    rest = frames - LANES
    first = LANES - rest
    shape = (LANES, LANES)
    row, lane = iota(shape, 0), iota(shape, 1)
    gap = jnp.zeros((first, LANES), f32)
    top = pk[:LANES]
    g11 = jnp.where(lane >= row, top, top.T)
    g21 = jnp.concatenate([pk[LANES:], gap], 0)
    low = jnp.concatenate([pk[first:LANES], gap], 0)
    low = jnp.where((lane <= row) & (row < rest), low, 0.0)
    g22 = jnp.where(lane <= row, low, low.T)
    return g11, g21.T, g21, g22


def spread(x, row):
    return jnp.broadcast_to(x[row : row + 1, :], (8, LANES))


def inverse_factor(a):
    count = K // 8
    sub, lane = iota((8, LANES), 0), iota((8, LANES), 1)
    base = (lane // K) * K
    rows = [a[8 * v : 8 * v + 8] for v in range(count)]
    inv = [jnp.where(sub + 8 * v == lane - base, 1.0, 0.0) for v in range(count)]
    for k0 in range(0, K, PANEL):
        cols = {
            k: {
                v: jnp.take_along_axis(rows[v], base + k, axis=1)
                for v in range(k0 // 8, count)
            }
            for k in range(k0, k0 + PANEL)
        }
        for j in range(k0, k0 + PANEL):
            vj, sj = j // 8, j % 8
            r = lax.rsqrt(spread(cols[j][vj], sj))
            fac = {v: cols[j][v] * r for v in range(vj, count)}
            fac[vj] = jnp.where(sub > sj, fac[vj], 0.0)
            for k in range(j + 1, k0 + PANEL):
                m = spread(fac[k // 8], k % 8)
                for v in range(k // 8, count):
                    cols[k][v] = cols[k][v] - fac[v] * m
            e = spread(inv[vj], sj) * r
            for v in range(vj, count):
                inv[v] = inv[v] - fac[v] * e
            inv[vj] = jnp.where(sub == sj, e, inv[vj])
            if k0 + PANEL < K:
                e = spread(rows[vj], sj) * r
                for v in range(vj, count):
                    rows[v] = rows[v] - fac[v] * e
    return jnp.concatenate(inv, 0)


def blockwise(parts_of):
    return jnp.concatenate([parts_of(b) for b in range(4)], 0)


def scalar_at(tile, lane_at):
    row, lane = iota(tile.shape, 0), iota(tile.shape, 1)
    return jnp.sum(jnp.where((row == 0) & (lane == lane_at), tile, 0.0)).astype(jnp.int32)


def subspaces(rows, cols, sums_ref, near_ref, far_ref, start_ref, high_ref, low_ref, z_ref, v_ref):
    row, col = lax.axis_index("gx"), lax.axis_index("gy")
    scale = 1.0 / float(BZ * BZ * BZ * 4)
    group = iota((K, LANES), 1) // K
    ranks, counts = [], []
    s_high, s_low = split(start_ref[...])
    s_both = jnp.concatenate([s_high, s_low], 0)
    for b in range(4):
        slot, turn_x = b % 2, b // 2
        other_ref = near_ref if turn_x == 0 else far_ref
        other = other_ref[slot]
        pk = (sums_ref[slot] + other.astype(f32)) * scale
        g11, g12, g21, g22 = unpacked(pk)
        for ref, part in ((high_ref, 0), (low_ref, 1)):
            ref[b, :LANES, :LANES] = split(g11)[part]
            ref[b, :LANES, LANES:] = split(g12)[part]
            ref[b, LANES:, :LANES] = split(g21)[part]
            ref[b, LANES:, LANES:] = split(g22)[part]
        right = lax.rem(col, 2) == slot
        down = lax.rem(row, 2) == turn_x
        tile = jnp.where(
            down,
            sums_ref[slot, META : META + 8, :],
            other_ref[slot, 0:16, :].astype(f32)[META : META + 8],
        )
        last_y = jnp.where(right, cols - 1, 0)
        last_x = jnp.where(down, rows - 1, 0)
        rank = jnp.where(col == last_y, 0, scalar_at(tile, 0))
        ranks.append(jnp.where(row == last_x, 0, rank))
        counts.append(scalar_at(tile, 1))
    for b in range(4):
        both = jnp.dot(s_both, high_ref[b], preferred_element_type=f32)
        z_ref[K * b : K * b + K, :] = (
            both[:K] + both[K:] + jnp.dot(s_high, low_ref[b], preferred_element_type=f32)
        )

    def turn(t, carry):
        z_high, z_low = split(z_ref[...])
        zz = jnp.concatenate([z_high, z_low], 0)
        s = lax.dot_general(zz, zz, (((1,), (1,)), ((), ())), preferred_element_type=f32)
        half = 4 * K
        s = (s[:half, :half] + s[half:, half:]) + (s[:half, half:] + s[half:, :half])
        a = jnp.where(group == 0, s[:K], 0.0)
        for b in range(1, 4):
            a = jnp.where(group == b, s[K * b : K * b + K], a)
        moved = []
        for b in range(4):
            high = z_high[K * b : K * b + K]
            low = z_low[K * b : K * b + K]
            both = jnp.dot(
                jnp.concatenate([high, low], 0), high_ref[b], preferred_element_type=f32
            )
            moved.append(
                both[:K] + both[K:] + jnp.dot(high, low_ref[b], preferred_element_type=f32)
            )
        y_high, y_low = split(jnp.concatenate(moved, 0))
        yy = jnp.concatenate([y_high, y_low], 0)
        inv = inverse_factor(a)
        wide = blockwise(lambda b: jnp.where(group == b, inv, 0.0))
        i_high, i_low = split(wide)
        left = jnp.concatenate(
            [jnp.concatenate([i_high, i_high], 1), jnp.concatenate([i_low, i_low], 1)], 0
        )
        nxt = jnp.dot(left, yy, preferred_element_type=f32)
        z_ref[...] = nxt[:half] + nxt[half:]
        v = jnp.dot(left, zz, preferred_element_type=f32)
        v = v[:half] + v[half:]
        for b in range(4):
            part = slice(K * b, K * b + K)

            @pl.when(counts[b] == t + 1)
            def _():
                v_ref[part, :] = v[part]

        return carry

    lax.fori_loop(0, ITERS, turn, 0)
    k = iota((K, v_ref.shape[1]), 0)
    return blockwise(lambda b: jnp.where(k < ranks[b], v_ref[K * b : K * b + K, :], 0.0)).astype(bf16)


def tents(rows, cols, span):
    row, col = lax.axis_index("gx"), lax.axis_index("gy")

    def share(far, position, at, last):
        first_edge = jnp.where(at == 0, 1.0, 0.0)
        last_edge = jnp.where(at == last, 1.0, 0.0)
        edge = jnp.maximum(first_edge, last_edge)
        tent = jnp.where(far, float(span) - position, position + 1.0) / float(span + 1)
        tent = tent * (1.0 - edge) + edge
        return tent * jnp.where(far, 1.0 - first_edge, 1.0 - last_edge)

    def along_x(offset):
        far = iota((8, LANES), 1) // (2 * K) != lax.rem(row, 2)
        return share(far, offset.astype(f32), row, rows - 1)

    group = iota((span, LANES), 1) // K
    far = group % 2 != lax.rem(col, 2)
    along_y = share(far, iota((span, LANES), 0).astype(f32), col, cols - 1)
    return along_x, along_y


def filter_kernel(
    rows, cols, span, sums_ref, near_ref, far_ref, start_ref, c_ref, out_ref, high_ref, low_ref, z_ref, v_ref, q_ref
):
    step = pl.program_id(0)
    frames = c_ref.shape[1]

    @pl.when(step == 0)
    def _():
        q_ref[...] = subspaces(
            rows, cols, sums_ref, near_ref, far_ref, start_ref, high_ref, low_ref, z_ref, v_ref
        )

    along_x, along_y = tents(rows, cols, span)
    q = q_ref[:, :frames]
    area = span * BZ
    per_step = c_ref.shape[0] // area
    for i in range(per_step):
        c = c_ref[i * area : (i + 1) * area, :]
        p = lax.dot_general(c, q, (((1,), (1,)), ((), ())), preferred_element_type=f32)
        wx = along_x(step * per_step + i)[:1]
        weight = along_y * wx
        p = p.reshape(span, BZ, LANES) * weight[:, None, :]
        p = p.reshape(area, LANES).astype(bf16)
        clutter = jnp.dot(p, q, preferred_element_type=f32)
        out_ref[i * area : (i + 1) * area, :] = (c.astype(f32) - clutter).astype(bf16)


def filtered(voxels, sums, near, far, start, rows, cols, span):
    m, frames = voxels.shape
    whole3 = pl.BlockSpec(sums.shape, lambda i: (0, 0, 0))
    chunk = pl.BlockSpec((PROJ_CHUNK, frames), lambda i: (i, 0))
    return pl.pallas_call(
        functools.partial(filter_kernel, rows, cols, span),
        grid=(m // PROJ_CHUNK,),
        in_specs=[whole3, whole3, whole3, pl.BlockSpec(start.shape, lambda i: (0, 0)), chunk],
        out_specs=chunk,
        out_shape=jax.ShapeDtypeStruct((m, frames), bf16),
        scratch_shapes=[
            pltpu.VMEM((4, 2 * LANES, 2 * LANES), bf16),
            pltpu.VMEM((4, 2 * LANES, 2 * LANES), bf16),
            pltpu.VMEM((4 * K, 2 * LANES), f32),
            pltpu.VMEM((4 * K, 2 * LANES), f32),
            pltpu.VMEM((4 * K, 2 * LANES), bf16),
        ],
        compiler_params=pltpu.CompilerParams(dimension_semantics=("arbitrary",)),
        cost_estimate=pl.CostEstimate(
            flops=8 * m * frames * K * 4, bytes_accessed=4 * m * frames, transcendentals=0
        ),
        name="filtered",
    )(sums, near, far, start, voxels)


def partner(x, axis):
    n = lax.axis_size(axis)
    return lax.ppermute(x, axis, [(i, i ^ 1) for i in range(n)])


def outer_partner(x, axis):
    n = lax.axis_size(axis)
    return lax.ppermute(x, axis, [(i, ((i - 1) ^ 1) + 1) for i in range(1, n - 1)])


def handed_on(x):
    n = lax.axis_size("gy")
    route = [(i, i + 2) for i in range(0, n - 2, 2)] + [(i, i - 2) for i in range(3, n, 2)]
    return lax.ppermute(x, "gy", route)


def body(echoes, start, ranks, counts):
    span, _, depth, frames = echoes.shape
    rows, cols = lax.axis_size("gx"), lax.axis_size("gy")
    voxels = echoes.reshape(span * span * depth, frames)
    own, sent = own_gram(voxels, ranks.reshape(1), counts.reshape(1))
    near = partner(sent, "gy")
    far = handed_on(near)
    even = lax.rem(lax.axis_index("gy"), 2) == 0
    near32, far32 = near.astype(f32), far.astype(f32)
    pair = jnp.stack([own + near32, own + far32])
    meta = jnp.stack([jnp.where(even, own, near32), jnp.where(even, far32, own)])
    at = (iota(pair.shape, 1) == META) & (iota(pair.shape, 2) < 2)
    pair = jnp.where(at, meta, pair)
    sent = pair.astype(bf16)
    near = partner(sent, "gx")
    far = outer_partner(sent, "gx")
    basis = jnp.pad(start.T, ((0, 0), (0, 2 * LANES - frames)))
    out = filtered(voxels, pair, near, far, basis, rows, cols, span)
    return out.reshape(echoes.shape)


def solution(mesh):
    placed = (P("gx", "gy", None, None), P(), P("gx", "gy", None), P("gx", "gy", None))
    return jax.shard_map(
        body, mesh=mesh, in_specs=placed, out_specs=P("gx", "gy", None, None), check_vma=False
    )
```

time: 89 us -> 44 us (0.49); the launches traced: 87.3 us -> 43.5 us
  other arithmetic: 28 us -> 1.72 us
  matrix products: 23 us -> 0 us
  Pallas kernels: 0 us -> 16.5 us
  starting transfers between devices: 24.7 us -> 15.6 us
  waiting for transfers between devices: 9.75 us -> 7.12 us
  local copies, waits for them, and re-layouts: 0.3 us -> 1.3 us
    another operation x22 -> x1, other arithmetic: 26.7 us -> 0.93 us  [body(): jnp.stack([jnp.where(even, own, near32), jnp.where(even, far32, own)])]
    dot_general x13 -> x0, matrix products: 22 us -> none  [the longest x4 17.1 us: add_block(): jnp.einsum('xyzk,fk->xyzf', coeff, vectors, preferred_element_type=jnp.fl...]
    pallas_call x0 -> x2, Pallas kernels: none -> 16.5 us  [the longest x1 12.5 us: filtered(): pl.pallas_call(functools.partial(filter_kernel, rows, cols, span), grid=(...]
    ppermute x4, starting transfers between devices: 24.7 us -> 15.6 us  [the longest x1 6.37 us: outer_partner(): lax.ppermute(x, axis, [(i, (i - 1 ^ 1) + 1) for i in range(1, n - 1)])]
    ppermute x4, waiting for transfers between devices: 9.75 us -> 7.12 us  [the longest x1 3.82 us: handed_on(): return lax.ppermute(x, 'gy', route)]
    mul x3 -> x0, other arithmetic: 1.06 us -> none  [the longest x2 0.99 us: project_quarter(): tent(jnp.arange(span_x, dtype=jnp.float32) + start_x, float(2 * span_x))]
    another operation x4 -> x0, matrix products: 0.99 us -> none  [subspace(): lax.linalg.triangular_solve(factor, moved, left_side=False, lower=True, t...]
  transfers between devices with their start and end apart: 4 -> 4, of which waited for: 3 -> 3; matrix products, arithmetic and copies ran while one was open for 9% -> 1% of each run, Pallas kernels for 0% -> 0%
where the time goes in v1:
time: 44 us; the launch traced here: 43.5 us
  Pallas kernels  16.5 us (38%)
  starting transfers between devices  15.6 us (35%)
  waiting for transfers between devices  7.12 us (16%)
  other arithmetic  1.72 us (4%)
  between operations  1.36 us (3%)
  local copies, waits for them, and re-layouts  1.3 us (3%)
    pallas_call x1, Pallas kernels, filtered(): pl.pallas_call(functools.partial(filter_kernel, rows, cols, span), grid=(...  12.5 us
    ppermute x1, starting transfers between devices, outer_partner(): lax.ppermute(x, axis, [(i, (i - 1 ^ 1) + 1) for i in range(1, n - 1)])  6.37 us
    ppermute x2, starting transfers between devices, partner(): return lax.ppermute(x, axis, [(i, i ^ 1) for i in range(n)])  6.1 us
    pallas_call x1, Pallas kernels, own_gram(): pl.pallas_call(gram_kernel, grid=(steps,), in_specs=[pl.BlockSpec(memory_...  3.92 us
    ppermute x1, waiting for transfers between devices, handed_on(): return lax.ppermute(x, 'gy', route)  3.82 us
    ppermute x1, starting transfers between devices, handed_on(): return lax.ppermute(x, 'gy', route)  3.11 us
    ppermute x2, waiting for transfers between devices, partner(): return lax.ppermute(x, axis, [(i, i ^ 1) for i in range(n)])  1.71 us
    ppermute x1, waiting for transfers between devices, outer_partner(): lax.ppermute(x, axis, [(i, (i - 1 ^ 1) + 1) for i in range(1, n - 1)])  1.59 us
  transfers between devices with their start and end apart: 4, of which 3 were waited for; matrix products, arithmetic and copies ran while one was open for 1% of the time, Pallas kernels for 0%

profile of v1, /device:TPU:49, one launch (start us, length us, event | category | flops | bytes accessed | tf_op | source)
XLA Modules:
  0.0 43.5 jit_solution(6385419041893190423)
XLA Ops:
  0.0 0.0 copy-start.2
  1.3 3.9 %own_gram.1 = (f32[200,128]{1,0:T(8,128)}, bf16[200,128]{1,0:T(8,128)(2,1)}) custom-call(s32[1]{0:T(128)} %bitcast.13.rank_ref, s32[1]{0:T(128)} %bitcast.14.count_ref, bf16[4096,200]{1,0:T(8,128)(2,1)} %bitcast.15), custom_call_target="tpu_custom_call" | custom-call | flops 327680000 | bytes 1638400 | tf_op jit(solution)/shard_map/own_gram/pallas_call | solution.py:64
  5.2 6.0 %collective-permute-start = (bf16[200,128]{1,0:T(8,128)(2,1)}, bf16[200,128]{1,0:T(8,128)(2,1)S(1)}, u32[]{:S(2)}, u32[]{:S(2)}) collective-permute-start(bf16[200,128]{1,0:T(8,128)(2,1)} %get-tuple-element.8), channel_id=1, source_target_pairs={{0,1},{1,0},{2,3},{3,2},{4,5},{5,4},{6,7},{7,6},{8,9},{9,8},{10,11... | collective-permute-start | bytes 153608 | tf_op jit(solution)/shard_map/ppermute | solution.py:314
  11.2 1.7 %collective-permute-done = bf16[200,128]{1,0:T(8,128)(2,1)S(1)} collective-permute-done((bf16[200,128]{1,0:T(8,128)(2,1)}, bf16[200,128]{1,0:T(8,128)(2,1)S(1)}, u32[]{:S(2)}, u32[]{:S(2)}) %collective-permute-start) | collective-permute-done | bytes 51232 | tf_op jit(solution)/shard_map/ppermute | solution.py:314
  12.9 3.1 %collective-permute-start.1 = (bf16[200,128]{1,0:T(8,128)(2,1)S(1)}, bf16[200,128]{1,0:T(8,128)(2,1)S(1)}, u32[]{:S(2)}, u32[]{:S(2)}) collective-permute-start(bf16[200,128]{1,0:T(8,128)(2,1)S(1)} %collective-permute-done), channel_id=1, source_target_pairs={{0,2},{2,4},{4,6},{6,8},{8,10},{10,12},{12,14},{14,16},{16,18},{18... | collective-permute-start | bytes 153608 | tf_op jit(solution)/shard_map/ppermute | solution.py:325
  16.1 3.8 %collective-permute-done.1 = bf16[200,128]{1,0:T(8,128)(2,1)S(1)} collective-permute-done((bf16[200,128]{1,0:T(8,128)(2,1)S(1)}, bf16[200,128]{1,0:T(8,128)(2,1)S(1)}, u32[]{:S(2)}, u32[]{:S(2)}) %collective-permute-start.1) | collective-permute-done | bytes 51232 | tf_op jit(solution)/shard_map/ppermute | solution.py:325
  19.9 0.9 %fusion = (f32[1,200,128]{2,1,0:T(8,128)S(1)}, f32[1,200,128]{2,1,0:T(8,128)S(1)}, f32[1,200,128]{2,1,0:T(8,128)S(1)}, f32[1,200,128]{2,1,0:T(8,128)S(1)}) fusion(f32[200,128]{1,0:T(8,128)} %get-tuple-element.7, bf16[200,128]{1,0:T(8,128)(2,1)S(1)} %collective-permute-done, pred[]{:T(512)S(6)} %eq.12, bf16[200,128]{1,0:T(8,128)(2,1)S(1)} %collective-permute-done.1), kind=kLoop, calls=%fused_computation.5 | loop fusion | flops 153600 | bytes 614401 | tf_op jit(solution)/shard_map/stack | solution.py:338
  20.8 0.8 %fusion.4 = (bf16[2,200,128]{2,1,0:T(8,128)(2,1)S(1)}, f32[2,200,128]{2,1,0:T(8,128)}) fusion(f32[1,200,128]{2,1,0:T(8,128)S(1)} %get-tuple-element.15, f32[1,200,128]{2,1,0:T(8,128)S(1)} %get-tuple-element.12, f32[1,200,128]{2,1,0:T(8,128)S(1)} %get-tuple-element.16, f32[1,200,128]{2,1,0:T(8,128)S(1)} %get-tuple-element.11, ...), kind=kLoop, calls=%fused_computation.11 | loop fusion | flops 256000 | bytes 717128 | tf_op jit(solution)/shard_map/convert_element_type | solution.py:341
  21.6 6.4 %collective-permute-start.3 = (bf16[2,200,128]{2,1,0:T(8,128)(2,1)S(1)}, bf16[2,200,128]{2,1,0:T(8,128)(2,1)S(1)}, u32[]{:S(2)}, u32[]{:S(2)}) collective-permute-start(bf16[2,200,128]{2,1,0:T(8,128)(2,1)S(1)} %get-tuple-element.9), channel_id=1, source_target_pairs={{32,64},{64,32},{96,128},{128,96},{160,192},{192,160},{33,65},{65,... | collective-permute-start | bytes 307208 | tf_op jit(solution)/shard_map/ppermute | solution.py:319
  28.0 0.1 collective-permute-start.2
  28.1 0.0 copy-done.2
  28.1 0.6 %pad.4.start_ref = f32[32,256]{1,0:T(8,128)} pad(f32[32,200]{1,0:T(8,128)S(1)} %bitcast.17, f32[]{:T(128)} %constant.15.clone.1), padding=0_0x0_56 | pad | bytes 58372 | tf_op jit(solution)/shard_map/jit(_pad)/pad | solution.py:344
  28.7 1.6 %collective-permute-done.3.far_ref = bf16[2,200,128]{2,1,0:T(8,128)(2,1)S(1)} collective-permute-done((bf16[2,200,128]{2,1,0:T(8,128)(2,1)S(1)}, bf16[2,200,128]{2,1,0:T(8,128)(2,1)S(1)}, u32[]{:S(2)}, u32[]{:S(2)}) %collective-permute-start.3) | collective-permute-done | bytes 102432 | tf_op jit(solution)/shard_map/ppermute | solution.py:319
  30.3 0.0 copy-start
  30.3 0.0 collective-permute-done.2.near_ref
  30.3 0.0 copy-start.1
  30.3 0.6 %copy-done = bf16[2,200,128]{2,1,0:T(8,128)(2,1)} copy-done((bf16[2,200,128]{2,1,0:T(8,128)(2,1)}, bf16[2,200,128]{2,1,0:T(8,128)(2,1)S(1)}, u32[]{:S(2)}) %copy-start) | copy-done | bytes 102424
  31.0 0.0 copy-done.1
  31.0 12.5 %filtered.1 = bf16[4096,200]{1,0:T(8,128)(2,1)} custom-call(f32[2,200,128]{2,1,0:T(8,128)} %get-tuple-element.10.sums_ref, bf16[2,200,128]{2,1,0:T(8,128)(2,1)} %copy-done.1, bf16[2,200,128]{2,1,0:T(8,128)(2,1)} %copy-done, f32[32,256]{1,0:T(8,128)} %pad.4.start_ref, bf16[4096,200]{1,0:T(8,128)(2,1)} %bitcast.16), custom_call_target="tpu_custom_call" | custom-call | flops 838860800 | bytes 3276800 | tf_op jit(solution)/shard_map/filtered/pallas_call | solution.py:291
  (2 shorter events, 0.0 us)
Async XLA Ops:
  0.0 28.1 %copy-start.2 = (f32[200,32]{0,1:T(8,128)S(1)}, f32[200,32]{0,1:T(8,128)}, u32[]{:S(2)}) copy-start(f32[200,32]{0,1:T(8,128)} %param.5) | copy-start | bytes 76804
  5.2 7.7 %collective-permute-start = (bf16[200,128]{1,0:T(8,128)(2,1)}, bf16[200,128]{1,0:T(8,128)(2,1)S(1)}, u32[]{:S(2)}, u32[]{:S(2)}) collective-permute-start(bf16[200,128]{1,0:T(8,128)(2,1)} %get-tuple-element.8), channel_id=1, source_target_pairs={{0,1},{1,0},{2,3},{3,2},{4,5},{5,4},{6,7},{7,6},{8,9},{9,8},{10,11... | collective-permute-start | bytes 153608 | tf_op jit(solution)/shard_map/ppermute | solution.py:314
  12.9 7.0 %collective-permute-start.1 = (bf16[200,128]{1,0:T(8,128)(2,1)S(1)}, bf16[200,128]{1,0:T(8,128)(2,1)S(1)}, u32[]{:S(2)}, u32[]{:S(2)}) collective-permute-start(bf16[200,128]{1,0:T(8,128)(2,1)S(1)} %collective-permute-done), channel_id=1, source_target_pairs={{0,2},{2,4},{4,6},{6,8},{8,10},{10,12},{12,14},{14,16},{16,18},{18... | collective-permute-start | bytes 153608 | tf_op jit(solution)/shard_map/ppermute | solution.py:325
  21.6 8.7 %collective-permute-start.3 = (bf16[2,200,128]{2,1,0:T(8,128)(2,1)S(1)}, bf16[2,200,128]{2,1,0:T(8,128)(2,1)S(1)}, u32[]{:S(2)}, u32[]{:S(2)}) collective-permute-start(bf16[2,200,128]{2,1,0:T(8,128)(2,1)S(1)} %get-tuple-element.9), channel_id=1, source_target_pairs={{32,64},{64,32},{96,128},{128,96},{160,192},{192,160},{33,65},{65,... | collective-permute-start | bytes 307208 | tf_op jit(solution)/shard_map/ppermute | solution.py:319
  28.0 2.3 %collective-permute-start.2 = (bf16[2,200,128]{2,1,0:T(8,128)(2,1)S(1)}, bf16[2,200,128]{2,1,0:T(8,128)(2,1)S(1)}, u32[]{:S(2)}, u32[]{:S(2)}) collective-permute-start(bf16[2,200,128]{2,1,0:T(8,128)(2,1)S(1)} %get-tuple-element.9), channel_id=1, source_target_pairs={{0,32},{32,0},{64,96},{96,64},{128,160},{160,128},{192,224},{224,1... | collective-permute-start | bytes 307208 | tf_op jit(solution)/shard_map/ppermute | solution.py:314
  30.3 0.6 %copy-start = (bf16[2,200,128]{2,1,0:T(8,128)(2,1)}, bf16[2,200,128]{2,1,0:T(8,128)(2,1)S(1)}, u32[]{:S(2)}) copy-start(bf16[2,200,128]{2,1,0:T(8,128)(2,1)S(1)} %collective-permute-done.3.far_ref) | copy-start | bytes 307204
  30.3 0.7 %copy-start.1 = (bf16[2,200,128]{2,1,0:T(8,128)(2,1)}, bf16[2,200,128]{2,1,0:T(8,128)(2,1)S(1)}, u32[]{:S(2)}) copy-start(bf16[2,200,128]{2,1,0:T(8,128)(2,1)S(1)} %collective-permute-done.2.near_ref) | copy-start | bytes 307204

commit v2 on v1

--- a/solution.py
+++ b/solution.py
@@ -14,6 +14,7 @@
 META = 8
 GRAM_CHUNK = 1024
 PROJ_CHUNK = 512
+VMEM_LIMIT = 56_000_000
 PANEL = 16
 
 f32 = jnp.float32
@@ -24,66 +25,110 @@
     return lax.broadcasted_iota(jnp.int32, shape, dim)
 
 
-def gram_kernel(rank_ref, count_ref, c_ref, own_ref, sent_ref, acc_ref):
-    step = pl.program_id(0)
-    frames = acc_ref.shape[0]
-    c = c_ref[...]
-    part = lax.dot_general(c, c, (((0,), (0,)), ((), ())), preferred_element_type=f32)
-
-    @pl.when(step == 0)
-    def _():
-        acc_ref[...] = part
-
-    @pl.when(step > 0)
-    def _():
-        acc_ref[...] += part
-
-    @pl.when(step == pl.num_programs(0) - 1)
-    def _():
-        rest = frames - LANES
-        first = LANES - rest
-        own_ref[...] = acc_ref[:, :LANES]
-        shape = (rest, rest)
-        low = iota(shape, 1) <= iota(shape, 0)
-        own_ref[first:LANES, :rest] = jnp.where(
-            low, acc_ref[LANES:, LANES:], acc_ref[first:LANES, :rest]
-        )
-        tile = own_ref[META : META + 8, :]
-        row, lane = iota(tile.shape, 0), iota(tile.shape, 1)
-        rank = rank_ref[0].astype(f32)
-        count = count_ref[0].astype(f32)
-        tile = jnp.where((row == 0) & (lane == 0), rank, tile)
-        tile = jnp.where((row == 0) & (lane == 1), count, tile)
-        own_ref[META : META + 8, :] = tile
-        sent_ref[...] = own_ref[...].astype(bf16)
+def gram_kernel(
+    rank_hbm, count_hbm, c_hbm, own_ref, sent_ref, rank_ref, count_ref, c_ref, acc_ref, sems, few_sems
+):
+    m, frames = c_ref.shape
+    few = [
+        pltpu.make_async_copy(rank_hbm, rank_ref, few_sems.at[0]),
+        pltpu.make_async_copy(count_hbm, count_ref, few_sems.at[1]),
+    ]
+    loads = []
+    for i in range(m // GRAM_CHUNK):
+        part = pl.ds(i * GRAM_CHUNK, GRAM_CHUNK)
+        loads.append(pltpu.make_async_copy(c_hbm.at[part], c_ref.at[part], sems.at[i]))
+        loads[-1].start()
+    for load in few:
+        load.start()
+    for i, load in enumerate(loads):
+        load.wait()
+        c = c_ref[i * GRAM_CHUNK : (i + 1) * GRAM_CHUNK, :]
+        part = lax.dot_general(c, c, (((0,), (0,)), ((), ())), preferred_element_type=f32)
+        if i == 0:
+            acc_ref[...] = part
+        else:
+            acc_ref[...] += part
+    for load in few:
+        load.wait()
+    rest = frames - LANES
+    first = LANES - rest
+    own_ref[...] = acc_ref[:, :LANES]
+    shape = (rest, rest)
+    low = iota(shape, 1) <= iota(shape, 0)
+    own_ref[first:LANES, :rest] = jnp.where(
+        low, acc_ref[LANES:, LANES:], acc_ref[first:LANES, :rest]
+    )
+    tile = own_ref[META : META + 8, :]
+    row, lane = iota(tile.shape, 0), iota(tile.shape, 1)
+    rank = jnp.broadcast_to(rank_ref[0].astype(f32), tile.shape)
+    count = jnp.broadcast_to(count_ref[0].astype(f32), tile.shape)
+    tile = jnp.where((row == 0) & (lane == 0), rank, tile)
+    tile = jnp.where((row == 0) & (lane == 1), count, tile)
+    own_ref[META : META + 8, :] = tile
+    sent_ref[...] = own_ref[...].astype(bf16)
+
+
+def vmem():
+    return pl.BlockSpec(memory_space=pltpu.VMEM)
+
+
+def hbm():
+    return pl.BlockSpec(memory_space=pltpu.HBM)
 
 
 def own_gram(voxels, rank, count):
     m, frames = voxels.shape
-    steps = m // GRAM_CHUNK
     return pl.pallas_call(
         gram_kernel,
-        grid=(steps,),
-        in_specs=[
-            pl.BlockSpec(memory_space=pltpu.SMEM),
-            pl.BlockSpec(memory_space=pltpu.SMEM),
-            pl.BlockSpec((GRAM_CHUNK, frames), lambda i: (i, 0)),
-        ],
-        out_specs=[
-            pl.BlockSpec((frames, LANES), lambda i: (0, 0)),
-            pl.BlockSpec((frames, LANES), lambda i: (0, 0)),
-        ],
+        in_specs=[hbm()] * 3,
+        out_specs=[vmem(), vmem()],
         out_shape=[
             jax.ShapeDtypeStruct((frames, LANES), f32),
             jax.ShapeDtypeStruct((frames, LANES), bf16),
         ],
-        scratch_shapes=[pltpu.VMEM((frames, frames), f32)],
-        compiler_params=pltpu.CompilerParams(dimension_semantics=("arbitrary",)),
+        scratch_shapes=[
+            pltpu.VMEM(rank.shape, jnp.int32),
+            pltpu.VMEM(count.shape, jnp.int32),
+            pltpu.VMEM((m, frames), bf16),
+            pltpu.VMEM((frames, frames), f32),
+            pltpu.SemaphoreType.DMA((m // GRAM_CHUNK,)),
+            pltpu.SemaphoreType.DMA((2,)),
+        ],
+        compiler_params=pltpu.CompilerParams(vmem_limit_bytes=VMEM_LIMIT),
         cost_estimate=pl.CostEstimate(
             flops=2 * m * frames * frames, bytes_accessed=2 * m * frames, transcendentals=0
         ),
         name="own_gram",
     )(rank, count, voxels)
+
+
+def pair_kernel(own_ref, near_ref, far_ref, pair_ref, sent_ref):
+    even = lax.rem(lax.axis_index("gy"), 2) == 0
+    own = own_ref[...]
+    at = slice(META, META + 8)
+    shape = (8, own.shape[1])
+    spot = (iota(shape, 0) == 0) & (iota(shape, 1) < 2)
+    for slot, other_ref in ((0, near_ref), (1, far_ref)):
+        other = other_ref[...].astype(f32)
+        total = own + other
+        pair_ref[slot] = total
+        right = even if slot == 0 else jnp.logical_not(even)
+        meta = jnp.where(right, own[at], other[at])
+        pair_ref[slot, at, :] = jnp.where(spot, meta, total[at])
+        sent_ref[slot] = pair_ref[slot].astype(bf16)
+
+
+def pair_sums(own, near, far):
+    shape = (2,) + own.shape
+    return pl.pallas_call(
+        pair_kernel,
+        in_specs=[vmem()] * 3,
+        out_specs=[vmem()] * 2,
+        out_shape=[jax.ShapeDtypeStruct(shape, f32), jax.ShapeDtypeStruct(shape, bf16)],
+        compiler_params=pltpu.CompilerParams(vmem_limit_bytes=VMEM_LIMIT),
+        cost_estimate=pl.CostEstimate(flops=4 * own.size, bytes_accessed=0, transcendentals=0),
+        name="pair_sums",
+    )(own, near, far)
 
 
 def split(x):
@@ -249,7 +294,7 @@
 
     def along_x(offset):
         far = iota((8, LANES), 1) // (2 * K) != lax.rem(row, 2)
-        return share(far, offset.astype(f32), row, rows - 1)
+        return share(far, offset, row, rows - 1)
 
     group = iota((span, LANES), 1) // K
     far = group % 2 != lax.rem(col, 2)
@@ -258,50 +303,74 @@
 
 
 def filter_kernel(
-    rows, cols, span, sums_ref, near_ref, far_ref, start_ref, c_ref, out_ref, high_ref, low_ref, z_ref, v_ref, q_ref
+    rows,
+    cols,
+    span,
+    sums_ref,
+    near_ref,
+    far_ref,
+    start_ref,
+    c_hbm,
+    out_hbm,
+    high_ref,
+    low_ref,
+    z_ref,
+    v_ref,
+    c_ref,
+    out_ref,
+    in_sems,
+    out_sems,
 ):
-    step = pl.program_id(0)
-    frames = c_ref.shape[1]
-
-    @pl.when(step == 0)
-    def _():
-        q_ref[...] = subspaces(
-            rows, cols, sums_ref, near_ref, far_ref, start_ref, high_ref, low_ref, z_ref, v_ref
-        )
-
+    m, frames = c_ref.shape
+    chunks = [pl.ds(i * PROJ_CHUNK, PROJ_CHUNK) for i in range(m // PROJ_CHUNK)]
+    loads = [
+        pltpu.make_async_copy(c_hbm.at[part], c_ref.at[part], in_sems.at[i])
+        for i, part in enumerate(chunks)
+    ]
+    stores = [
+        pltpu.make_async_copy(out_ref.at[part], out_hbm.at[part], out_sems.at[i])
+        for i, part in enumerate(chunks)
+    ]
+    for load in loads:
+        load.start()
+    q = subspaces(rows, cols, sums_ref, near_ref, far_ref, start_ref, high_ref, low_ref, z_ref, v_ref)
+    q = q[:, :frames]
     along_x, along_y = tents(rows, cols, span)
-    q = q_ref[:, :frames]
     area = span * BZ
-    per_step = c_ref.shape[0] // area
-    for i in range(per_step):
-        c = c_ref[i * area : (i + 1) * area, :]
+    for load in loads:
+        load.wait()
+    for at in range(0, m, area):
+        c = c_ref[at : at + area, :]
         p = lax.dot_general(c, q, (((1,), (1,)), ((), ())), preferred_element_type=f32)
-        wx = along_x(step * per_step + i)[:1]
-        weight = along_y * wx
+        weight = along_y * along_x(float(at // area))[:1]
         p = p.reshape(span, BZ, LANES) * weight[:, None, :]
         p = p.reshape(area, LANES).astype(bf16)
         clutter = jnp.dot(p, q, preferred_element_type=f32)
-        out_ref[i * area : (i + 1) * area, :] = (c.astype(f32) - clutter).astype(bf16)
+        out_ref[at : at + area, :] = (c.astype(f32) - clutter).astype(bf16)
+        if (at + area) % PROJ_CHUNK == 0:
+            stores[at // PROJ_CHUNK].start()
+    for store in stores:
+        store.wait()
 
 
 def filtered(voxels, sums, near, far, start, rows, cols, span):
     m, frames = voxels.shape
-    whole3 = pl.BlockSpec(sums.shape, lambda i: (0, 0, 0))
-    chunk = pl.BlockSpec((PROJ_CHUNK, frames), lambda i: (i, 0))
     return pl.pallas_call(
         functools.partial(filter_kernel, rows, cols, span),
-        grid=(m // PROJ_CHUNK,),
-        in_specs=[whole3, whole3, whole3, pl.BlockSpec(start.shape, lambda i: (0, 0)), chunk],
-        out_specs=chunk,
+        in_specs=[vmem()] * 4 + [hbm()],
+        out_specs=hbm(),
         out_shape=jax.ShapeDtypeStruct((m, frames), bf16),
         scratch_shapes=[
             pltpu.VMEM((4, 2 * LANES, 2 * LANES), bf16),
             pltpu.VMEM((4, 2 * LANES, 2 * LANES), bf16),
             pltpu.VMEM((4 * K, 2 * LANES), f32),
             pltpu.VMEM((4 * K, 2 * LANES), f32),
-            pltpu.VMEM((4 * K, 2 * LANES), bf16),
+            pltpu.VMEM((m, frames), bf16),
+            pltpu.VMEM((m, frames), bf16),
+            pltpu.SemaphoreType.DMA((m // PROJ_CHUNK,)),
+            pltpu.SemaphoreType.DMA((m // PROJ_CHUNK,)),
         ],
-        compiler_params=pltpu.CompilerParams(dimension_semantics=("arbitrary",)),
+        compiler_params=pltpu.CompilerParams(vmem_limit_bytes=VMEM_LIMIT),
         cost_estimate=pl.CostEstimate(
             flops=8 * m * frames * K * 4, bytes_accessed=4 * m * frames, transcendentals=0
         ),
@@ -329,16 +398,10 @@
     span, _, depth, frames = echoes.shape
     rows, cols = lax.axis_size("gx"), lax.axis_size("gy")
     voxels = echoes.reshape(span * span * depth, frames)
-    own, sent = own_gram(voxels, ranks.reshape(1), counts.reshape(1))
+    own, sent = own_gram(voxels, ranks, counts)
     near = partner(sent, "gy")
     far = handed_on(near)
-    even = lax.rem(lax.axis_index("gy"), 2) == 0
-    near32, far32 = near.astype(f32), far.astype(f32)
-    pair = jnp.stack([own + near32, own + far32])
-    meta = jnp.stack([jnp.where(even, own, near32), jnp.where(even, far32, own)])
-    at = (iota(pair.shape, 1) == META) & (iota(pair.shape, 2) < 2)
-    pair = jnp.where(at, meta, pair)
-    sent = pair.astype(bf16)
+    pair, sent = pair_sums(own, near, far)
     near = partner(sent, "gx")
     far = outer_partner(sent, "gx")
     basis = jnp.pad(start.T, ((0, 0), (0, 2 * LANES - frames)))

time: 44 us -> 34.8 us (0.79)
  Pallas kernels: 16.5 us -> 9.96 us
  other arithmetic: 1.72 us -> 0 us
  local copies, waits for them, and re-layouts: 1.3 us -> 0.01 us
    pallas_call x2 -> x3, Pallas kernels: 16.5 us -> 9.96 us  [the longest x1 7.18 us: filtered(): pl.pallas_call(functools.partial(filter_kernel, rows, cols, span), in_spe...]
    another operation x1 -> x0, other arithmetic: 0.93 us -> none  [body(): jnp.stack([jnp.where(even, own, near32), jnp.where(even, far32, own)])]
    convert_element_type x1 -> x0, other arithmetic: 0.78 us -> none  [body(): sent = pair.astype(bf16)]
    unnamed x6 -> x2, local copies, waits for them, and re-layouts: 0.67 us -> 0.01 us
    pad x1, local copies, waits for them, and re-layouts: 0.62 us -> 0.01 us  [body(): basis = jnp.pad(start.T, ((0, 0), (0, 2 * LANES - frames)))]
    ppermute x1, waiting for transfers between devices: 1.59 us -> 2.2 us  [outer_partner(): lax.ppermute(x, axis, [(i, (i - 1 ^ 1) + 1) for i in range(1, n - 1)])]
  transfers between devices with their start and end apart: 4 -> 4, of which waited for: 3 -> 3; matrix products, arithmetic and copies ran while one was open for 1% -> 0% of each run, Pallas kernels for 0% -> 0%
where the time goes in v2:
time: 34.8 us; the launch traced here: 34.6 us
  starting transfers between devices  15.7 us (45%)
  Pallas kernels  9.96 us (29%)
  waiting for transfers between devices  7.55 us (22%)
  between operations  1.36 us (4%)
    pallas_call x1, Pallas kernels, filtered(): pl.pallas_call(functools.partial(filter_kernel, rows, cols, span), in_spe...  7.18 us
    ppermute x1, starting transfers between devices, outer_partner(): lax.ppermute(x, axis, [(i, (i - 1 ^ 1) + 1) for i in range(1, n - 1)])  6.38 us
    ppermute x2, starting transfers between devices, partner(): return lax.ppermute(x, axis, [(i, i ^ 1) for i in range(n)])  6.19 us
    ppermute x1, waiting for transfers between devices, handed_on(): return lax.ppermute(x, 'gy', route)  3.84 us
    ppermute x1, starting transfers between devices, handed_on(): return lax.ppermute(x, 'gy', route)  3.11 us
    pallas_call x1, Pallas kernels, own_gram(): pl.pallas_call(gram_kernel, in_specs=[hbm()] * 3, out_specs=[vmem(), vmem...  2.75 us
    ppermute x1, waiting for transfers between devices, outer_partner(): lax.ppermute(x, axis, [(i, (i - 1 ^ 1) + 1) for i in range(1, n - 1)])  2.2 us
    ppermute x2, waiting for transfers between devices, partner(): return lax.ppermute(x, axis, [(i, i ^ 1) for i in range(n)])  1.5 us
  transfers between devices with their start and end apart: 4, of which 3 were waited for; matrix products, arithmetic and copies ran while one was open for 0% of the time, Pallas kernels for 0%

profile of v2, /device:TPU:49, one launch (start us, length us, event | category | flops | bytes accessed | tf_op | source)
XLA Modules:
  0.0 34.6 jit_solution(16434601637002761866)
XLA Ops:
  0.0 0.0 copy-start
  1.3 2.7 %own_gram.1 = (f32[200,128]{1,0:T(8,128)S(1)}, bf16[200,128]{1,0:T(8,128)(2,1)S(1)}) custom-call(s32[1,1,1]{2,1,0:T(1,128)S(6)} %copy.5.rank_hbm, s32[1,1,1]{2,1,0:T(1,128)S(6)} %copy.6.count_hbm, bf16[4096,200]{1,0:T(8,128)(2,1)} %bitcast.3), custom_call_target="tpu_custom_call" | custom-call | flops 327680000 | bytes 1638400 | tf_op jit(solution)/shard_map/own_gram/pallas_call | solution.py:81
  4.1 6.1 %collective-permute-start = (bf16[200,128]{1,0:T(8,128)(2,1)S(1)}, bf16[200,128]{1,0:T(8,128)(2,1)S(1)}, u32[]{:S(2)}, u32[]{:S(2)}) collective-permute-start(bf16[200,128]{1,0:T(8,128)(2,1)S(1)} %get-tuple-element.10), channel_id=1, source_target_pairs={{0,1},{1,0},{2,3},{3,2},{4,5},{5,4},{6,7},{7,6},{8,9},{9,8},{10,11... | collective-permute-start | bytes 153608 | tf_op jit(solution)/shard_map/ppermute | solution.py:383
  10.2 1.5 %collective-permute-done.near_ref = bf16[200,128]{1,0:T(8,128)(2,1)S(1)} collective-permute-done((bf16[200,128]{1,0:T(8,128)(2,1)S(1)}, bf16[200,128]{1,0:T(8,128)(2,1)S(1)}, u32[]{:S(2)}, u32[]{:S(2)}) %collective-permute-start) | collective-permute-done | bytes 51232 | tf_op jit(solution)/shard_map/ppermute | solution.py:383
  11.7 3.1 %collective-permute-start.1 = (bf16[200,128]{1,0:T(8,128)(2,1)S(1)}, bf16[200,128]{1,0:T(8,128)(2,1)S(1)}, u32[]{:S(2)}, u32[]{:S(2)}) collective-permute-start(bf16[200,128]{1,0:T(8,128)(2,1)S(1)} %collective-permute-done.near_ref), channel_id=1, source_target_pairs={{0,2},{2,4},{4,6},{6,8},{8,10},{10,12},{12,14},{14,16},{16,18},{18... | collective-permute-start | bytes 153608 | tf_op jit(solution)/shard_map/ppermute | solution.py:394
  14.8 3.8 %collective-permute-done.1.far_ref = bf16[200,128]{1,0:T(8,128)(2,1)S(1)} collective-permute-done((bf16[200,128]{1,0:T(8,128)(2,1)S(1)}, bf16[200,128]{1,0:T(8,128)(2,1)S(1)}, u32[]{:S(2)}, u32[]{:S(2)}) %collective-permute-start.1) | collective-permute-done | bytes 51232 | tf_op jit(solution)/shard_map/ppermute | solution.py:394
  18.6 6.4 %collective-permute-start.3 = (bf16[2,200,128]{2,1,0:T(8,128)(2,1)S(1)}, bf16[2,200,128]{2,1,0:T(8,128)(2,1)S(1)}, u32[]{:S(2)}, u32[]{:S(2)}) collective-permute-start(bf16[2,200,128]{2,1,0:T(8,128)(2,1)S(1)} %get-tuple-element.12), channel_id=1, source_target_pairs={{32,64},{64,32},{96,128},{128,96},{160,192},{192,160},{33,65},{65,... | collective-permute-start | bytes 307208 | tf_op jit(solution)/shard_map/ppermute | solution.py:388
  25.0 0.1 collective-permute-start.2
  25.1 0.0 copy-done
  25.2 2.2 %collective-permute-done.3.far_ref = bf16[2,200,128]{2,1,0:T(8,128)(2,1)S(1)} collective-permute-done((bf16[2,200,128]{2,1,0:T(8,128)(2,1)S(1)}, bf16[2,200,128]{2,1,0:T(8,128)(2,1)S(1)}, u32[]{:S(2)}, u32[]{:S(2)}) %collective-permute-start.3) | collective-permute-done | bytes 102432 | tf_op jit(solution)/shard_map/ppermute | solution.py:388
  27.4 0.0 collective-permute-done.2.near_ref
  27.4 7.2 %filtered.1 = bf16[4096,200]{1,0:T(8,128)(2,1)} custom-call(f32[2,200,128]{2,1,0:T(8,128)S(1)} %get-tuple-element.11.sums_ref, bf16[2,200,128]{2,1,0:T(8,128)(2,1)S(1)} %collective-permute-done.2.near_ref, bf16[2,200,128]{2,1,0:T(8,128)(2,1)S(1)} %collective-permute-done.3.far_ref, f32[32,256]{1,0:T(8,128)S(1)} %pad.4.start_ref, bf16[4096,200]{1,0:T(8,128)(2,1)} %bitcast.4), custom_call_target="tpu_custom_call" | custom-call | flops 838860800 | bytes 3276800 | tf_op jit(solution)/shard_map/filtered/pallas_call | solution.py:358
  (2 shorter events, 0.0 us)
Async XLA Ops:
  0.0 25.1 %copy-start = (f32[200,32]{0,1:T(8,128)S(1)}, f32[200,32]{0,1:T(8,128)}, u32[]{:S(2)}) copy-start(f32[200,32]{0,1:T(8,128)} %param.5) | copy-start | bytes 76804
  4.1 7.6 %collective-permute-start = (bf16[200,128]{1,0:T(8,128)(2,1)S(1)}, bf16[200,128]{1,0:T(8,128)(2,1)S(1)}, u32[]{:S(2)}, u32[]{:S(2)}) collective-permute-start(bf16[200,128]{1,0:T(8,128)(2,1)S(1)} %get-tuple-element.10), channel_id=1, source_target_pairs={{0,1},{1,0},{2,3},{3,2},{4,5},{5,4},{6,7},{7,6},{8,9},{9,8},{10,11... | collective-permute-start | bytes 153608 | tf_op jit(solution)/shard_map/ppermute | solution.py:383
  11.7 7.0 %collective-permute-start.1 = (bf16[200,128]{1,0:T(8,128)(2,1)S(1)}, bf16[200,128]{1,0:T(8,128)(2,1)S(1)}, u32[]{:S(2)}, u32[]{:S(2)}) collective-permute-start(bf16[200,128]{1,0:T(8,128)(2,1)S(1)} %collective-permute-done.near_ref), channel_id=1, source_target_pairs={{0,2},{2,4},{4,6},{6,8},{8,10},{10,12},{12,14},{14,16},{16,18},{18... | collective-permute-start | bytes 153608 | tf_op jit(solution)/shard_map/ppermute | solution.py:394
  18.6 8.7 %collective-permute-start.3 = (bf16[2,200,128]{2,1,0:T(8,128)(2,1)S(1)}, bf16[2,200,128]{2,1,0:T(8,128)(2,1)S(1)}, u32[]{:S(2)}, u32[]{:S(2)}) collective-permute-start(bf16[2,200,128]{2,1,0:T(8,128)(2,1)S(1)} %get-tuple-element.12), channel_id=1, source_target_pairs={{32,64},{64,32},{96,128},{128,96},{160,192},{192,160},{33,65},{65,... | collective-permute-start | bytes 307208 | tf_op jit(solution)/shard_map/ppermute | solution.py:388
  25.0 2.3 %collective-permute-start.2 = (bf16[2,200,128]{2,1,0:T(8,128)(2,1)S(1)}, bf16[2,200,128]{2,1,0:T(8,128)(2,1)S(1)}, u32[]{:S(2)}, u32[]{:S(2)}) collective-permute-start(bf16[2,200,128]{2,1,0:T(8,128)(2,1)S(1)} %get-tuple-element.12), channel_id=1, source_target_pairs={{0,32},{32,0},{64,96},{96,64},{128,160},{160,128},{192,224},{224,1... | collective-permute-start | bytes 307208 | tf_op jit(solution)/shard_map/ppermute | solution.py:383

commit v3 on v2

--- a/solution.py
+++ b/solution.py
@@ -12,9 +12,10 @@
 ITERS = 4
 LANES = 128
 META = 8
-GRAM_CHUNK = 1024
+LOAD_ROWS = 512
+GRAM_ROWS = (2560, 1536)
 PROJ_CHUNK = 512
-VMEM_LIMIT = 56_000_000
+VMEM_LIMIT = 55_500_000
 PANEL = 16
 
 f32 = jnp.float32
@@ -25,31 +26,24 @@
     return lax.broadcasted_iota(jnp.int32, shape, dim)
 
 
-def gram_kernel(
-    rank_hbm, count_hbm, c_hbm, own_ref, sent_ref, rank_ref, count_ref, c_ref, acc_ref, sems, few_sems
-):
+def gram_kernel(c_hbm, own_ref, c_ref, acc_ref, sems):
     m, frames = c_ref.shape
-    few = [
-        pltpu.make_async_copy(rank_hbm, rank_ref, few_sems.at[0]),
-        pltpu.make_async_copy(count_hbm, count_ref, few_sems.at[1]),
-    ]
     loads = []
-    for i in range(m // GRAM_CHUNK):
-        part = pl.ds(i * GRAM_CHUNK, GRAM_CHUNK)
+    for i in range(m // LOAD_ROWS):
+        part = pl.ds(i * LOAD_ROWS, LOAD_ROWS)
         loads.append(pltpu.make_async_copy(c_hbm.at[part], c_ref.at[part], sems.at[i]))
         loads[-1].start()
-    for load in few:
-        load.start()
-    for i, load in enumerate(loads):
-        load.wait()
-        c = c_ref[i * GRAM_CHUNK : (i + 1) * GRAM_CHUNK, :]
+    first = 0
+    for i, size in enumerate(GRAM_ROWS):
+        for load in loads[first // LOAD_ROWS : (first + size) // LOAD_ROWS]:
+            load.wait()
+        c = c_ref[first : first + size, :]
         part = lax.dot_general(c, c, (((0,), (0,)), ((), ())), preferred_element_type=f32)
         if i == 0:
             acc_ref[...] = part
         else:
             acc_ref[...] += part
-    for load in few:
-        load.wait()
+        first += size
     rest = frames - LANES
     first = LANES - rest
     own_ref[...] = acc_ref[:, :LANES]
@@ -58,14 +52,6 @@
     own_ref[first:LANES, :rest] = jnp.where(
         low, acc_ref[LANES:, LANES:], acc_ref[first:LANES, :rest]
     )
-    tile = own_ref[META : META + 8, :]
-    row, lane = iota(tile.shape, 0), iota(tile.shape, 1)
-    rank = jnp.broadcast_to(rank_ref[0].astype(f32), tile.shape)
-    count = jnp.broadcast_to(count_ref[0].astype(f32), tile.shape)
-    tile = jnp.where((row == 0) & (lane == 0), rank, tile)
-    tile = jnp.where((row == 0) & (lane == 1), count, tile)
-    own_ref[META : META + 8, :] = tile
-    sent_ref[...] = own_ref[...].astype(bf16)
 
 
 def vmem():
@@ -76,35 +62,30 @@
     return pl.BlockSpec(memory_space=pltpu.HBM)
 
 
-def own_gram(voxels, rank, count):
+def own_gram(voxels):
     m, frames = voxels.shape
     return pl.pallas_call(
         gram_kernel,
-        in_specs=[hbm()] * 3,
-        out_specs=[vmem(), vmem()],
-        out_shape=[
-            jax.ShapeDtypeStruct((frames, LANES), f32),
-            jax.ShapeDtypeStruct((frames, LANES), bf16),
-        ],
+        in_specs=[hbm()],
+        out_specs=vmem(),
+        out_shape=jax.ShapeDtypeStruct((frames, LANES), f32),
         scratch_shapes=[
-            pltpu.VMEM(rank.shape, jnp.int32),
-            pltpu.VMEM(count.shape, jnp.int32),
             pltpu.VMEM((m, frames), bf16),
             pltpu.VMEM((frames, frames), f32),
-            pltpu.SemaphoreType.DMA((m // GRAM_CHUNK,)),
-            pltpu.SemaphoreType.DMA((2,)),
+            pltpu.SemaphoreType.DMA((m // LOAD_ROWS,)),
         ],
         compiler_params=pltpu.CompilerParams(vmem_limit_bytes=VMEM_LIMIT),
         cost_estimate=pl.CostEstimate(
             flops=2 * m * frames * frames, bytes_accessed=2 * m * frames, transcendentals=0
         ),
         name="own_gram",
-    )(rank, count, voxels)
-
-
-def pair_kernel(own_ref, near_ref, far_ref, pair_ref, sent_ref):
+    )(voxels)
+
+
+def pair_kernel(own_ref, mine_ref, near_ref, far_ref, pair_ref, sent_ref):
     even = lax.rem(lax.axis_index("gy"), 2) == 0
     own = own_ref[...]
+    mine = mine_ref[0:16, :].astype(f32)
     at = slice(META, META + 8)
     shape = (8, own.shape[1])
     spot = (iota(shape, 0) == 0) & (iota(shape, 1) < 2)
@@ -113,22 +94,22 @@
         total = own + other
         pair_ref[slot] = total
         right = even if slot == 0 else jnp.logical_not(even)
-        meta = jnp.where(right, own[at], other[at])
+        meta = jnp.where(right, mine[at], other[at])
         pair_ref[slot, at, :] = jnp.where(spot, meta, total[at])
         sent_ref[slot] = pair_ref[slot].astype(bf16)
 
 
-def pair_sums(own, near, far):
+def pair_sums(own, mine, near, far):
     shape = (2,) + own.shape
     return pl.pallas_call(
         pair_kernel,
-        in_specs=[vmem()] * 3,
+        in_specs=[vmem()] * 4,
         out_specs=[vmem()] * 2,
         out_shape=[jax.ShapeDtypeStruct(shape, f32), jax.ShapeDtypeStruct(shape, bf16)],
         compiler_params=pltpu.CompilerParams(vmem_limit_bytes=VMEM_LIMIT),
         cost_estimate=pl.CostEstimate(flops=4 * own.size, bytes_accessed=0, transcendentals=0),
         name="pair_sums",
-    )(own, near, far)
+    )(own, mine, near, far)
 
 
 def split(x):
@@ -195,11 +176,6 @@
     return jnp.concatenate([parts_of(b) for b in range(4)], 0)
 
 
-def scalar_at(tile, lane_at):
-    row, lane = iota(tile.shape, 0), iota(tile.shape, 1)
-    return jnp.sum(jnp.where((row == 0) & (lane == lane_at), tile, 0.0)).astype(jnp.int32)
-
-
 def subspaces(rows, cols, sums_ref, near_ref, far_ref, start_ref, high_ref, low_ref, z_ref, v_ref):
     row, col = lax.axis_index("gx"), lax.axis_index("gy")
     scale = 1.0 / float(BZ * BZ * BZ * 4)
@@ -227,9 +203,10 @@
         )
         last_y = jnp.where(right, cols - 1, 0)
         last_x = jnp.where(down, rows - 1, 0)
-        rank = jnp.where(col == last_y, 0, scalar_at(tile, 0))
-        ranks.append(jnp.where(row == last_x, 0, rank))
-        counts.append(scalar_at(tile, 1))
+        there = jnp.where(col == last_y, 0.0, 1.0) * jnp.where(row == last_x, 0.0, 1.0)
+        wide = (K, v_ref.shape[1])
+        ranks.append(jnp.broadcast_to(tile[:1, 0:1] * there, wide))
+        counts.append(jnp.broadcast_to(tile[:1, 1:2], wide))
     for b in range(4):
         both = jnp.dot(s_both, high_ref[b], preferred_element_type=f32)
         z_ref[K * b : K * b + K, :] = (
@@ -267,17 +244,14 @@
         z_ref[...] = nxt[:half] + nxt[half:]
         v = jnp.dot(left, zz, preferred_element_type=f32)
         v = v[:half] + v[half:]
+        turns = (t + 1).astype(f32)
         for b in range(4):
             part = slice(K * b, K * b + K)
-
-            @pl.when(counts[b] == t + 1)
-            def _():
-                v_ref[part, :] = v[part]
-
+            v_ref[part, :] = jnp.where(counts[b] == turns, v[part], v_ref[part, :])
         return carry
 
     lax.fori_loop(0, ITERS, turn, 0)
-    k = iota((K, v_ref.shape[1]), 0)
+    k = iota((K, v_ref.shape[1]), 0).astype(f32)
     return blockwise(lambda b: jnp.where(k < ranks[b], v_ref[K * b : K * b + K, :], 0.0)).astype(bf16)
 
 
@@ -398,10 +372,14 @@
     span, _, depth, frames = echoes.shape
     rows, cols = lax.axis_size("gx"), lax.axis_size("gy")
     voxels = echoes.reshape(span * span * depth, frames)
-    own, sent = own_gram(voxels, ranks, counts)
-    near = partner(sent, "gy")
+    own = own_gram(voxels)
+    own, ranks, counts = lax.optimization_barrier((own, ranks, counts))
+    row, lane = iota(own.shape, 0), iota(own.shape, 1)
+    rank = jnp.where((row == META) & (lane == 0), ranks[0, 0, 0].astype(f32), own)
+    mine = jnp.where((row == META) & (lane == 1), counts[0, 0, 0].astype(f32), rank).astype(bf16)
+    near = partner(mine, "gy")
     far = handed_on(near)
-    pair, sent = pair_sums(own, near, far)
+    pair, sent = pair_sums(own, mine, near, far)
     near = partner(sent, "gx")
     far = outer_partner(sent, "gx")
     basis = jnp.pad(start.T, ((0, 0), (0, 2 * LANES - frames)))

time: 34.8 us -> 34.6 us (level)
  no operation moved by 1% of the time
where the time goes in v3:
time: 34.6 us; the launch traced here: 34.3 us
  starting transfers between devices  15.7 us (45%)
  Pallas kernels  9.63 us (28%)
  waiting for transfers between devices  7.55 us (22%)
  between operations  1.38 us (4%)
    pallas_call x1, Pallas kernels, filtered(): pl.pallas_call(functools.partial(filter_kernel, rows, cols, span), in_spe...  7.13 us
    ppermute x1, starting transfers between devices, outer_partner(): lax.ppermute(x, axis, [(i, (i - 1 ^ 1) + 1) for i in range(1, n - 1)])  6.38 us
    ppermute x2, starting transfers between devices, partner(): return lax.ppermute(x, axis, [(i, i ^ 1) for i in range(n)])  6.19 us
    ppermute x1, waiting for transfers between devices, handed_on(): return lax.ppermute(x, 'gy', route)  3.84 us
    ppermute x1, starting transfers between devices, handed_on(): return lax.ppermute(x, 'gy', route)  3.11 us
    pallas_call x1, Pallas kernels, own_gram(): pl.pallas_call(gram_kernel, in_specs=[hbm()], out_specs=vmem(), out_shape...  2.47 us
    ppermute x1, waiting for transfers between devices, outer_partner(): lax.ppermute(x, axis, [(i, (i - 1 ^ 1) + 1) for i in range(1, n - 1)])  2.2 us
    ppermute x2, waiting for transfers between devices, partner(): return lax.ppermute(x, axis, [(i, i ^ 1) for i in range(n)])  1.5 us
  transfers between devices with their start and end apart: 4, of which 3 were waited for; matrix products, arithmetic and copies ran while one was open for 0% of the time, Pallas kernels for 0%

profile of v3, /device:TPU:49, one launch (start us, length us, event | category | flops | bytes accessed | tf_op | source)
XLA Modules:
  0.0 34.3 jit_solution(9031957119856473142)
XLA Ops:
  0.0 0.0 copy-start
  1.3 2.5 %own_gram.1.own_ref = f32[200,128]{1,0:T(8,128)S(1)} custom-call(bf16[4096,200]{1,0:T(8,128)(2,1)} %bitcast.5), custom_call_target="tpu_custom_call" | custom-call | flops 327680000 | bytes 1638400 | tf_op jit(solution)/shard_map/own_gram/pallas_call | solution.py:67
  3.8 0.1 select_convert_fusion.mine_ref
  3.9 6.1 %collective-permute-start = (bf16[200,128]{1,0:T(8,128)(2,1)S(1)}, bf16[200,128]{1,0:T(8,128)(2,1)S(1)}, u32[]{:S(2)}, u32[]{:S(2)}) collective-permute-start(bf16[200,128]{1,0:T(8,128)(2,1)S(1)} %select_convert_fusion.mine_ref), channel_id=1, source_target_pairs={{0,1},{1,0},{2,3},{3,2},{4,5},{5,4},{6,7},{7,6},{8,9},{9,8},{10,11... | collective-permute-start | bytes 153608 | tf_op jit(solution)/shard_map/ppermute | solution.py:357
  10.0 1.5 %collective-permute-done.near_ref = bf16[200,128]{1,0:T(8,128)(2,1)S(1)} collective-permute-done((bf16[200,128]{1,0:T(8,128)(2,1)S(1)}, bf16[200,128]{1,0:T(8,128)(2,1)S(1)}, u32[]{:S(2)}, u32[]{:S(2)}) %collective-permute-start) | collective-permute-done | bytes 51232 | tf_op jit(solution)/shard_map/ppermute | solution.py:357
  11.5 3.1 %collective-permute-start.1 = (bf16[200,128]{1,0:T(8,128)(2,1)S(1)}, bf16[200,128]{1,0:T(8,128)(2,1)S(1)}, u32[]{:S(2)}, u32[]{:S(2)}) collective-permute-start(bf16[200,128]{1,0:T(8,128)(2,1)S(1)} %collective-permute-done.near_ref), channel_id=1, source_target_pairs={{0,2},{2,4},{4,6},{6,8},{8,10},{10,12},{12,14},{14,16},{16,18},{18... | collective-permute-start | bytes 153608 | tf_op jit(solution)/shard_map/ppermute | solution.py:368
  14.6 3.8 %collective-permute-done.1.far_ref = bf16[200,128]{1,0:T(8,128)(2,1)S(1)} collective-permute-done((bf16[200,128]{1,0:T(8,128)(2,1)S(1)}, bf16[200,128]{1,0:T(8,128)(2,1)S(1)}, u32[]{:S(2)}, u32[]{:S(2)}) %collective-permute-start.1) | collective-permute-done | bytes 51232 | tf_op jit(solution)/shard_map/ppermute | solution.py:368
  18.5 6.4 %collective-permute-start.3 = (bf16[2,200,128]{2,1,0:T(8,128)(2,1)S(1)}, bf16[2,200,128]{2,1,0:T(8,128)(2,1)S(1)}, u32[]{:S(2)}, u32[]{:S(2)}) collective-permute-start(bf16[2,200,128]{2,1,0:T(8,128)(2,1)S(1)} %get-tuple-element.14), channel_id=1, source_target_pairs={{32,64},{64,32},{96,128},{128,96},{160,192},{192,160},{33,65},{65,... | collective-permute-start | bytes 307208 | tf_op jit(solution)/shard_map/ppermute | solution.py:362
  24.9 0.1 collective-permute-start.2
  25.0 0.0 copy-done
  25.0 2.2 %collective-permute-done.3.far_ref = bf16[2,200,128]{2,1,0:T(8,128)(2,1)S(1)} collective-permute-done((bf16[2,200,128]{2,1,0:T(8,128)(2,1)S(1)}, bf16[2,200,128]{2,1,0:T(8,128)(2,1)S(1)}, u32[]{:S(2)}, u32[]{:S(2)}) %collective-permute-start.3) | collective-permute-done | bytes 102432 | tf_op jit(solution)/shard_map/ppermute | solution.py:362
  27.2 0.0 collective-permute-done.2.near_ref
  27.2 7.1 %filtered.1 = bf16[4096,200]{1,0:T(8,128)(2,1)} custom-call(f32[2,200,128]{2,1,0:T(8,128)S(1)} %get-tuple-element.13.sums_ref, bf16[2,200,128]{2,1,0:T(8,128)(2,1)S(1)} %collective-permute-done.2.near_ref, bf16[2,200,128]{2,1,0:T(8,128)(2,1)S(1)} %collective-permute-done.3.far_ref, f32[32,256]{1,0:T(8,128)S(1)} %pad.4.start_ref, bf16[4096,200]{1,0:T(8,128)(2,1)} %bitcast.6), custom_call_target="tpu_custom_call" | custom-call | flops 838860800 | bytes 3276800 | tf_op jit(solution)/shard_map/filtered/pallas_call | solution.py:332
  (4 shorter events, 0.0 us)
Async XLA Ops:
  0.0 25.0 %copy-start = (f32[200,32]{0,1:T(8,128)S(1)}, f32[200,32]{0,1:T(8,128)}, u32[]{:S(2)}) copy-start(f32[200,32]{0,1:T(8,128)} %param.5) | copy-start | bytes 76804
  3.9 7.6 %collective-permute-start = (bf16[200,128]{1,0:T(8,128)(2,1)S(1)}, bf16[200,128]{1,0:T(8,128)(2,1)S(1)}, u32[]{:S(2)}, u32[]{:S(2)}) collective-permute-start(bf16[200,128]{1,0:T(8,128)(2,1)S(1)} %select_convert_fusion.mine_ref), channel_id=1, source_target_pairs={{0,1},{1,0},{2,3},{3,2},{4,5},{5,4},{6,7},{7,6},{8,9},{9,8},{10,11... | collective-permute-start | bytes 153608 | tf_op jit(solution)/shard_map/ppermute | solution.py:357
  11.5 7.0 %collective-permute-start.1 = (bf16[200,128]{1,0:T(8,128)(2,1)S(1)}, bf16[200,128]{1,0:T(8,128)(2,1)S(1)}, u32[]{:S(2)}, u32[]{:S(2)}) collective-permute-start(bf16[200,128]{1,0:T(8,128)(2,1)S(1)} %collective-permute-done.near_ref), channel_id=1, source_target_pairs={{0,2},{2,4},{4,6},{6,8},{8,10},{10,12},{12,14},{14,16},{16,18},{18... | collective-permute-start | bytes 153608 | tf_op jit(solution)/shard_map/ppermute | solution.py:368
  18.5 8.7 %collective-permute-start.3 = (bf16[2,200,128]{2,1,0:T(8,128)(2,1)S(1)}, bf16[2,200,128]{2,1,0:T(8,128)(2,1)S(1)}, u32[]{:S(2)}, u32[]{:S(2)}) collective-permute-start(bf16[2,200,128]{2,1,0:T(8,128)(2,1)S(1)} %get-tuple-element.14), channel_id=1, source_target_pairs={{32,64},{64,32},{96,128},{128,96},{160,192},{192,160},{33,65},{65,... | collective-permute-start | bytes 307208 | tf_op jit(solution)/shard_map/ppermute | solution.py:362
  24.9 2.3 %collective-permute-start.2 = (bf16[2,200,128]{2,1,0:T(8,128)(2,1)S(1)}, bf16[2,200,128]{2,1,0:T(8,128)(2,1)S(1)}, u32[]{:S(2)}, u32[]{:S(2)}) collective-permute-start(bf16[2,200,128]{2,1,0:T(8,128)(2,1)S(1)} %get-tuple-element.14), channel_id=1, source_target_pairs={{0,32},{32,0},{64,96},{96,64},{128,160},{160,128},{192,224},{224,1... | collective-permute-start | bytes 307208 | tf_op jit(solution)/shard_map/ppermute | solution.py:357

commit v4 on v3

--- a/solution.py
+++ b/solution.py
@@ -12,10 +12,9 @@
 ITERS = 4
 LANES = 128
 META = 8
-LOAD_ROWS = 512
-GRAM_ROWS = (2560, 1536)
 PROJ_CHUNK = 512
-VMEM_LIMIT = 55_500_000
+VMEM_LIMIT = 24 * 1024 * 1024
+META_FLOPS = 1_000_000_000
 PANEL = 16
 
 f32 = jnp.float32
@@ -26,24 +25,30 @@
     return lax.broadcasted_iota(jnp.int32, shape, dim)
 
 
-def gram_kernel(c_hbm, own_ref, c_ref, acc_ref, sems):
-    m, frames = c_ref.shape
-    loads = []
-    for i in range(m // LOAD_ROWS):
-        part = pl.ds(i * LOAD_ROWS, LOAD_ROWS)
-        loads.append(pltpu.make_async_copy(c_hbm.at[part], c_ref.at[part], sems.at[i]))
-        loads[-1].start()
-    first = 0
-    for i, size in enumerate(GRAM_ROWS):
-        for load in loads[first // LOAD_ROWS : (first + size) // LOAD_ROWS]:
-            load.wait()
-        c = c_ref[first : first + size, :]
-        part = lax.dot_general(c, c, (((0,), (0,)), ((), ())), preferred_element_type=f32)
-        if i == 0:
-            acc_ref[...] = part
-        else:
-            acc_ref[...] += part
-        first += size
+def meta_kernel(rank_ref, count_ref, meta_ref):
+    shape = meta_ref.shape
+    row, lane = iota(shape, 0), iota(shape, 1)
+    rank, count = rank_ref[0, 0, 0].astype(f32), count_ref[0, 0, 0].astype(f32)
+    meta = jnp.where(lane == 0, rank, jnp.where(lane == 1, count, 0.0))
+    meta_ref[...] = jnp.where(row == 0, meta, 0.0)
+
+
+def meta_tile(rank, count):
+    return pl.pallas_call(
+        meta_kernel,
+        in_specs=[pl.BlockSpec(memory_space=pltpu.SMEM)] * 2,
+        out_specs=vmem(),
+        out_shape=jax.ShapeDtypeStruct((8, LANES), f32),
+        compiler_params=pltpu.CompilerParams(vmem_limit_bytes=VMEM_LIMIT),
+        cost_estimate=pl.CostEstimate(flops=META_FLOPS, bytes_accessed=0, transcendentals=0),
+        name="meta_tile",
+    )(rank, count)
+
+
+def gram_kernel(meta_ref, c_ref, own_ref, sent_ref, acc_ref):
+    frames = c_ref.shape[1]
+    c = c_ref[...]
+    acc_ref[...] = lax.dot_general(c, c, (((0,), (0,)), ((), ())), preferred_element_type=f32)
     rest = frames - LANES
     first = LANES - rest
     own_ref[...] = acc_ref[:, :LANES]
@@ -52,6 +57,10 @@
     own_ref[first:LANES, :rest] = jnp.where(
         low, acc_ref[LANES:, LANES:], acc_ref[first:LANES, :rest]
     )
+    tile = own_ref[META : META + 8, :]
+    spot = (iota(tile.shape, 0) == 0) & (iota(tile.shape, 1) < 2)
+    own_ref[META : META + 8, :] = jnp.where(spot, meta_ref[...], tile)
+    sent_ref[...] = own_ref[...].astype(bf16)
 
 
 def vmem():
@@ -62,24 +71,23 @@
     return pl.BlockSpec(memory_space=pltpu.HBM)
 
 
-def own_gram(voxels):
+def own_gram(voxels, meta):
     m, frames = voxels.shape
     return pl.pallas_call(
         gram_kernel,
-        in_specs=[hbm()],
-        out_specs=vmem(),
-        out_shape=jax.ShapeDtypeStruct((frames, LANES), f32),
-        scratch_shapes=[
-            pltpu.VMEM((m, frames), bf16),
-            pltpu.VMEM((frames, frames), f32),
-            pltpu.SemaphoreType.DMA((m // LOAD_ROWS,)),
+        in_specs=[vmem()] * 2,
+        out_specs=[vmem()] * 2,
+        out_shape=[
+            jax.ShapeDtypeStruct((frames, LANES), f32),
+            jax.ShapeDtypeStruct((frames, LANES), bf16),
         ],
+        scratch_shapes=[pltpu.VMEM((frames, frames), f32)],
         compiler_params=pltpu.CompilerParams(vmem_limit_bytes=VMEM_LIMIT),
         cost_estimate=pl.CostEstimate(
             flops=2 * m * frames * frames, bytes_accessed=2 * m * frames, transcendentals=0
         ),
         name="own_gram",
-    )(voxels)
+    )(meta, voxels)
 
 
 def pair_kernel(own_ref, mine_ref, near_ref, far_ref, pair_ref, sent_ref):
@@ -284,35 +292,25 @@
     near_ref,
     far_ref,
     start_ref,
-    c_hbm,
+    c_ref,
     out_hbm,
     high_ref,
     low_ref,
     z_ref,
     v_ref,
-    c_ref,
     out_ref,
-    in_sems,
     out_sems,
 ):
     m, frames = c_ref.shape
     chunks = [pl.ds(i * PROJ_CHUNK, PROJ_CHUNK) for i in range(m // PROJ_CHUNK)]
-    loads = [
-        pltpu.make_async_copy(c_hbm.at[part], c_ref.at[part], in_sems.at[i])
-        for i, part in enumerate(chunks)
-    ]
     stores = [
         pltpu.make_async_copy(out_ref.at[part], out_hbm.at[part], out_sems.at[i])
         for i, part in enumerate(chunks)
     ]
-    for load in loads:
-        load.start()
     q = subspaces(rows, cols, sums_ref, near_ref, far_ref, start_ref, high_ref, low_ref, z_ref, v_ref)
     q = q[:, :frames]
     along_x, along_y = tents(rows, cols, span)
     area = span * BZ
-    for load in loads:
-        load.wait()
     for at in range(0, m, area):
         c = c_ref[at : at + area, :]
         p = lax.dot_general(c, q, (((1,), (1,)), ((), ())), preferred_element_type=f32)
@@ -331,7 +329,7 @@
     m, frames = voxels.shape
     return pl.pallas_call(
         functools.partial(filter_kernel, rows, cols, span),
-        in_specs=[vmem()] * 4 + [hbm()],
+        in_specs=[vmem()] * 5,
         out_specs=hbm(),
         out_shape=jax.ShapeDtypeStruct((m, frames), bf16),
         scratch_shapes=[
@@ -340,8 +338,6 @@
             pltpu.VMEM((4 * K, 2 * LANES), f32),
             pltpu.VMEM((4 * K, 2 * LANES), f32),
             pltpu.VMEM((m, frames), bf16),
-            pltpu.VMEM((m, frames), bf16),
-            pltpu.SemaphoreType.DMA((m // PROJ_CHUNK,)),
             pltpu.SemaphoreType.DMA((m // PROJ_CHUNK,)),
         ],
         compiler_params=pltpu.CompilerParams(vmem_limit_bytes=VMEM_LIMIT),
@@ -372,11 +368,7 @@
     span, _, depth, frames = echoes.shape
     rows, cols = lax.axis_size("gx"), lax.axis_size("gy")
     voxels = echoes.reshape(span * span * depth, frames)
-    own = own_gram(voxels)
-    own, ranks, counts = lax.optimization_barrier((own, ranks, counts))
-    row, lane = iota(own.shape, 0), iota(own.shape, 1)
-    rank = jnp.where((row == META) & (lane == 0), ranks[0, 0, 0].astype(f32), own)
-    mine = jnp.where((row == META) & (lane == 1), counts[0, 0, 0].astype(f32), rank).astype(bf16)
+    own, mine = own_gram(voxels, meta_tile(ranks, counts))
     near = partner(mine, "gy")
     far = handed_on(near)
     pair, sent = pair_sums(own, mine, near, far)

time: 34.6 us -> 33 us (0.954)
  Pallas kernels: 9.63 us -> 7.93 us
    pallas_call x1 -> x2, Pallas kernels: 2.47 us -> 0.87 us  [the longest x1 0.86 us: own_gram(): pl.pallas_call(gram_kernel, in_specs=[vmem()] * 2, out_specs=[vmem()] * 2...]
where the time goes in v4:
time: 33 us; the launch traced here: 32.8 us
  starting transfers between devices  15.7 us (48%)
  Pallas kernels  7.93 us (24%)
  waiting for transfers between devices  7.54 us (23%)
  between operations  1.51 us (5%)
    pallas_call x1, Pallas kernels, filtered(): pl.pallas_call(functools.partial(filter_kernel, rows, cols, span), in_spe...  7.03 us
    ppermute x1, starting transfers between devices, outer_partner(): lax.ppermute(x, axis, [(i, (i - 1 ^ 1) + 1) for i in range(1, n - 1)])  6.38 us
    ppermute x2, starting transfers between devices, partner(): return lax.ppermute(x, axis, [(i, i ^ 1) for i in range(n)])  6.19 us
    ppermute x1, waiting for transfers between devices, handed_on(): return lax.ppermute(x, 'gy', route)  3.84 us
    ppermute x1, starting transfers between devices, handed_on(): return lax.ppermute(x, 'gy', route)  3.11 us
    ppermute x1, waiting for transfers between devices, outer_partner(): lax.ppermute(x, axis, [(i, (i - 1 ^ 1) + 1) for i in range(1, n - 1)])  2.2 us
    ppermute x2, waiting for transfers between devices, partner(): return lax.ppermute(x, axis, [(i, i ^ 1) for i in range(n)])  1.5 us
    pallas_call x1, Pallas kernels, own_gram(): pl.pallas_call(gram_kernel, in_specs=[vmem()] * 2, out_specs=[vmem()] * 2...  0.86 us
  transfers between devices with their start and end apart: 4, of which 3 were waited for; matrix products, arithmetic and copies ran while one was open for 0% of the time, Pallas kernels for 0%

profile of v4, /device:TPU:49, one launch (start us, length us, event | category | flops | bytes accessed | tf_op | source)
XLA Modules:
  0.0 32.8 jit_solution(9028191951556838606)
XLA Ops:
  0.0 0.0 copy-start
  1.5 0.0 copy-start.1
  1.5 0.1 copy-done
  1.6 0.9 %own_gram.1 = (f32[200,128]{1,0:T(8,128)S(1)}, bf16[200,128]{1,0:T(8,128)(2,1)S(1)}) custom-call(f32[8,128]{1,0:T(8,128)S(1)} %meta_tile.1.meta_ref, bf16[4096,200]{1,0:T(8,128)(2,1)S(1)} %bitcast.3), custom_call_target="tpu_custom_call" | custom-call | flops 327680000 | bytes 1638400 | tf_op jit(solution)/shard_map/own_gram/pallas_call | solution.py:76
  2.5 6.1 %collective-permute-start = (bf16[200,128]{1,0:T(8,128)(2,1)S(1)}, bf16[200,128]{1,0:T(8,128)(2,1)S(1)}, u32[]{:S(2)}, u32[]{:S(2)}) collective-permute-start(bf16[200,128]{1,0:T(8,128)(2,1)S(1)} %get-tuple-element.10.mine_ref), channel_id=1, source_target_pairs={{0,1},{1,0},{2,3},{3,2},{4,5},{5,4},{6,7},{7,6},{8,9},{9,8},{10,11... | collective-permute-start | bytes 153608 | tf_op jit(solution)/shard_map/ppermute | solution.py:353
  8.6 1.5 %collective-permute-done.near_ref = bf16[200,128]{1,0:T(8,128)(2,1)S(1)} collective-permute-done((bf16[200,128]{1,0:T(8,128)(2,1)S(1)}, bf16[200,128]{1,0:T(8,128)(2,1)S(1)}, u32[]{:S(2)}, u32[]{:S(2)}) %collective-permute-start) | collective-permute-done | bytes 51232 | tf_op jit(solution)/shard_map/ppermute | solution.py:353
  10.1 3.1 %collective-permute-start.1 = (bf16[200,128]{1,0:T(8,128)(2,1)S(1)}, bf16[200,128]{1,0:T(8,128)(2,1)S(1)}, u32[]{:S(2)}, u32[]{:S(2)}) collective-permute-start(bf16[200,128]{1,0:T(8,128)(2,1)S(1)} %collective-permute-done.near_ref), channel_id=1, source_target_pairs={{0,2},{2,4},{4,6},{6,8},{8,10},{10,12},{12,14},{14,16},{16,18},{18... | collective-permute-start | bytes 153608 | tf_op jit(solution)/shard_map/ppermute | solution.py:364
  13.2 3.8 %collective-permute-done.1.far_ref = bf16[200,128]{1,0:T(8,128)(2,1)S(1)} collective-permute-done((bf16[200,128]{1,0:T(8,128)(2,1)S(1)}, bf16[200,128]{1,0:T(8,128)(2,1)S(1)}, u32[]{:S(2)}, u32[]{:S(2)}) %collective-permute-start.1) | collective-permute-done | bytes 51232 | tf_op jit(solution)/shard_map/ppermute | solution.py:364
  17.1 6.4 %collective-permute-start.3 = (bf16[2,200,128]{2,1,0:T(8,128)(2,1)S(1)}, bf16[2,200,128]{2,1,0:T(8,128)(2,1)S(1)}, u32[]{:S(2)}, u32[]{:S(2)}) collective-permute-start(bf16[2,200,128]{2,1,0:T(8,128)(2,1)S(1)} %get-tuple-element.12), channel_id=1, source_target_pairs={{32,64},{64,32},{96,128},{128,96},{160,192},{192,160},{33,65},{65,... | collective-permute-start | bytes 307208 | tf_op jit(solution)/shard_map/ppermute | solution.py:358
  23.4 0.1 collective-permute-start.2
  23.5 0.0 copy-done.1
  23.6 2.2 %collective-permute-done.3.far_ref = bf16[2,200,128]{2,1,0:T(8,128)(2,1)S(1)} collective-permute-done((bf16[2,200,128]{2,1,0:T(8,128)(2,1)S(1)}, bf16[2,200,128]{2,1,0:T(8,128)(2,1)S(1)}, u32[]{:S(2)}, u32[]{:S(2)}) %collective-permute-start.3) | collective-permute-done | bytes 102432 | tf_op jit(solution)/shard_map/ppermute | solution.py:358
  25.8 0.0 collective-permute-done.2.near_ref
  25.8 7.0 %filtered.1 = bf16[4096,200]{1,0:T(8,128)(2,1)} custom-call(f32[2,200,128]{2,1,0:T(8,128)S(1)} %get-tuple-element.11.sums_ref, bf16[2,200,128]{2,1,0:T(8,128)(2,1)S(1)} %collective-permute-done.2.near_ref, bf16[2,200,128]{2,1,0:T(8,128)(2,1)S(1)} %collective-permute-done.3.far_ref, f32[32,256]{1,0:T(8,128)S(1)} %pad.4.start_ref, bf16[4096,200]{1,0:T(8,128)(2,1)S(1)} %bitcast.4), custom_call_target="tpu_custom_call" | custom-call | flops 838860800 | bytes 3276800 | tf_op jit(solution)/shard_map/filtered/pallas_call | solution.py:330
  (3 shorter events, 0.0 us)
Async XLA Ops:
  0.0 1.6 %copy-start = (bf16[16,16,16,200]{3,2,1,0:T(8,128)(2,1)S(1)}, bf16[16,16,16,200]{3,2,1,0:T(8,128)(2,1)}, u32[]{:S(2)}) copy-start(bf16[16,16,16,200]{3,2,1,0:T(8,128)(2,1)} %param.4) | copy-start | bytes 4915204
  1.5 22.1 %copy-start.1 = (f32[200,32]{0,1:T(8,128)S(1)}, f32[200,32]{0,1:T(8,128)}, u32[]{:S(2)}) copy-start(f32[200,32]{0,1:T(8,128)} %param.5) | copy-start | bytes 76804
  2.5 7.6 %collective-permute-start = (bf16[200,128]{1,0:T(8,128)(2,1)S(1)}, bf16[200,128]{1,0:T(8,128)(2,1)S(1)}, u32[]{:S(2)}, u32[]{:S(2)}) collective-permute-start(bf16[200,128]{1,0:T(8,128)(2,1)S(1)} %get-tuple-element.10.mine_ref), channel_id=1, source_target_pairs={{0,1},{1,0},{2,3},{3,2},{4,5},{5,4},{6,7},{7,6},{8,9},{9,8},{10,11... | collective-permute-start | bytes 153608 | tf_op jit(solution)/shard_map/ppermute | solution.py:353
  10.1 7.0 %collective-permute-start.1 = (bf16[200,128]{1,0:T(8,128)(2,1)S(1)}, bf16[200,128]{1,0:T(8,128)(2,1)S(1)}, u32[]{:S(2)}, u32[]{:S(2)}) collective-permute-start(bf16[200,128]{1,0:T(8,128)(2,1)S(1)} %collective-permute-done.near_ref), channel_id=1, source_target_pairs={{0,2},{2,4},{4,6},{6,8},{8,10},{10,12},{12,14},{14,16},{16,18},{18... | collective-permute-start | bytes 153608 | tf_op jit(solution)/shard_map/ppermute | solution.py:364
  17.1 8.7 %collective-permute-start.3 = (bf16[2,200,128]{2,1,0:T(8,128)(2,1)S(1)}, bf16[2,200,128]{2,1,0:T(8,128)(2,1)S(1)}, u32[]{:S(2)}, u32[]{:S(2)}) collective-permute-start(bf16[2,200,128]{2,1,0:T(8,128)(2,1)S(1)} %get-tuple-element.12), channel_id=1, source_target_pairs={{32,64},{64,32},{96,128},{128,96},{160,192},{192,160},{33,65},{65,... | collective-permute-start | bytes 307208 | tf_op jit(solution)/shard_map/ppermute | solution.py:358
  23.4 2.3 %collective-permute-start.2 = (bf16[2,200,128]{2,1,0:T(8,128)(2,1)S(1)}, bf16[2,200,128]{2,1,0:T(8,128)(2,1)S(1)}, u32[]{:S(2)}, u32[]{:S(2)}) collective-permute-start(bf16[2,200,128]{2,1,0:T(8,128)(2,1)S(1)} %get-tuple-element.12), channel_id=1, source_target_pairs={{0,32},{32,0},{64,96},{96,64},{128,160},{160,128},{192,224},{224,1... | collective-permute-start | bytes 307208 | tf_op jit(solution)/shard_map/ppermute | solution.py:353

commit v5 on v4

--- a/solution.py
+++ b/solution.py
@@ -15,7 +15,7 @@
 PROJ_CHUNK = 512
 VMEM_LIMIT = 24 * 1024 * 1024
 META_FLOPS = 1_000_000_000
-PANEL = 16
+PANELS = (0, 20, K)
 
 f32 = jnp.float32
 bf16 = jnp.bfloat16
@@ -152,20 +152,20 @@
     base = (lane // K) * K
     rows = [a[8 * v : 8 * v + 8] for v in range(count)]
     inv = [jnp.where(sub + 8 * v == lane - base, 1.0, 0.0) for v in range(count)]
-    for k0 in range(0, K, PANEL):
+    for k0, k1 in zip(PANELS, PANELS[1:]):
         cols = {
             k: {
                 v: jnp.take_along_axis(rows[v], base + k, axis=1)
                 for v in range(k0 // 8, count)
             }
-            for k in range(k0, k0 + PANEL)
+            for k in range(k0, k1)
         }
-        for j in range(k0, k0 + PANEL):
+        for j in range(k0, k1):
             vj, sj = j // 8, j % 8
             r = lax.rsqrt(spread(cols[j][vj], sj))
             fac = {v: cols[j][v] * r for v in range(vj, count)}
             fac[vj] = jnp.where(sub > sj, fac[vj], 0.0)
-            for k in range(j + 1, k0 + PANEL):
+            for k in range(j + 1, k1):
                 m = spread(fac[k // 8], k % 8)
                 for v in range(k // 8, count):
                     cols[k][v] = cols[k][v] - fac[v] * m
@@ -173,7 +173,7 @@
             for v in range(vj, count):
                 inv[v] = inv[v] - fac[v] * e
             inv[vj] = jnp.where(sub == sj, e, inv[vj])
-            if k0 + PANEL < K:
+            if k1 < K:
                 e = spread(rows[vj], sj) * r
                 for v in range(vj, count):
                     rows[v] = rows[v] - fac[v] * e
@@ -184,13 +184,12 @@
     return jnp.concatenate([parts_of(b) for b in range(4)], 0)
 
 
-def subspaces(rows, cols, sums_ref, near_ref, far_ref, start_ref, high_ref, low_ref, z_ref, v_ref):
+def subspaces(rows, cols, sums_ref, near_ref, far_ref, start_ref, high_ref, low_ref, v_ref):
     row, col = lax.axis_index("gx"), lax.axis_index("gy")
     scale = 1.0 / float(BZ * BZ * BZ * 4)
     group = iota((K, LANES), 1) // K
     ranks, counts = [], []
     s_high, s_low = split(start_ref[...])
-    s_both = jnp.concatenate([s_high, s_low], 0)
     for b in range(4):
         slot, turn_x = b % 2, b // 2
         other_ref = near_ref if turn_x == 0 else far_ref
@@ -215,50 +214,39 @@
         wide = (K, v_ref.shape[1])
         ranks.append(jnp.broadcast_to(tile[:1, 0:1] * there, wide))
         counts.append(jnp.broadcast_to(tile[:1, 1:2], wide))
-    for b in range(4):
-        both = jnp.dot(s_both, high_ref[b], preferred_element_type=f32)
-        z_ref[K * b : K * b + K, :] = (
-            both[:K] + both[K:] + jnp.dot(s_high, low_ref[b], preferred_element_type=f32)
-        )
-
-    def turn(t, carry):
-        z_high, z_low = split(z_ref[...])
+    def moved(high, low, b):
+        both = jnp.dot(jnp.concatenate([high, low], 0), high_ref[b], preferred_element_type=f32)
+        return both[:K] + both[K:] + jnp.dot(high, low_ref[b], preferred_element_type=f32)
+
+    half = 4 * K
+    z = blockwise(lambda b: moved(s_high, s_low, b))
+    for t in range(ITERS):
+        z_high, z_low = split(z)
         zz = jnp.concatenate([z_high, z_low], 0)
         s = lax.dot_general(zz, zz, (((1,), (1,)), ((), ())), preferred_element_type=f32)
-        half = 4 * K
         s = (s[:half, :half] + s[half:, half:]) + (s[:half, half:] + s[half:, :half])
         a = jnp.where(group == 0, s[:K], 0.0)
         for b in range(1, 4):
             a = jnp.where(group == b, s[K * b : K * b + K], a)
-        moved = []
-        for b in range(4):
-            high = z_high[K * b : K * b + K]
-            low = z_low[K * b : K * b + K]
-            both = jnp.dot(
-                jnp.concatenate([high, low], 0), high_ref[b], preferred_element_type=f32
-            )
-            moved.append(
-                both[:K] + both[K:] + jnp.dot(high, low_ref[b], preferred_element_type=f32)
-            )
-        y_high, y_low = split(jnp.concatenate(moved, 0))
-        yy = jnp.concatenate([y_high, y_low], 0)
         inv = inverse_factor(a)
         wide = blockwise(lambda b: jnp.where(group == b, inv, 0.0))
         i_high, i_low = split(wide)
         left = jnp.concatenate(
             [jnp.concatenate([i_high, i_high], 1), jnp.concatenate([i_low, i_low], 1)], 0
         )
-        nxt = jnp.dot(left, yy, preferred_element_type=f32)
-        z_ref[...] = nxt[:half] + nxt[half:]
+        if t < ITERS - 1:
+            parts = [slice(K * b, K * b + K) for b in range(4)]
+            y = blockwise(lambda b: moved(z_high[parts[b]], z_low[parts[b]], b))
+            nxt = jnp.dot(left, jnp.concatenate(split(y), 0), preferred_element_type=f32)
+            z = nxt[:half] + nxt[half:]
         v = jnp.dot(left, zz, preferred_element_type=f32)
         v = v[:half] + v[half:]
-        turns = (t + 1).astype(f32)
         for b in range(4):
             part = slice(K * b, K * b + K)
-            v_ref[part, :] = jnp.where(counts[b] == turns, v[part], v_ref[part, :])
-        return carry
-
-    lax.fori_loop(0, ITERS, turn, 0)
+            if t == 0:
+                v_ref[part, :] = v[part]
+            else:
+                v_ref[part, :] = jnp.where(counts[b] > t, v[part], v_ref[part, :])
     k = iota((K, v_ref.shape[1]), 0).astype(f32)
     return blockwise(lambda b: jnp.where(k < ranks[b], v_ref[K * b : K * b + K, :], 0.0)).astype(bf16)
 
@@ -296,7 +284,6 @@
     out_hbm,
     high_ref,
     low_ref,
-    z_ref,
     v_ref,
     out_ref,
     out_sems,
@@ -307,7 +294,7 @@
         pltpu.make_async_copy(out_ref.at[part], out_hbm.at[part], out_sems.at[i])
         for i, part in enumerate(chunks)
     ]
-    q = subspaces(rows, cols, sums_ref, near_ref, far_ref, start_ref, high_ref, low_ref, z_ref, v_ref)
+    q = subspaces(rows, cols, sums_ref, near_ref, far_ref, start_ref, high_ref, low_ref, v_ref)
     q = q[:, :frames]
     along_x, along_y = tents(rows, cols, span)
     area = span * BZ
@@ -336,7 +323,6 @@
             pltpu.VMEM((4, 2 * LANES, 2 * LANES), bf16),
             pltpu.VMEM((4, 2 * LANES, 2 * LANES), bf16),
             pltpu.VMEM((4 * K, 2 * LANES), f32),
-            pltpu.VMEM((4 * K, 2 * LANES), f32),
             pltpu.VMEM((m, frames), bf16),
             pltpu.SemaphoreType.DMA((m // PROJ_CHUNK,)),
         ],

time: 33 us -> 32.5 us (0.985)
  Pallas kernels: 7.93 us -> 7.43 us
    pallas_call x1, Pallas kernels: 7.03 us -> 6.53 us  [filtered(): pl.pallas_call(functools.partial(filter_kernel, rows, cols, span), in_spe...]
where the time goes in v5:
time: 32.5 us; the launch traced here: 32.3 us
  starting transfers between devices  15.7 us (48%)
  waiting for transfers between devices  7.54 us (23%)
  Pallas kernels  7.43 us (23%)
  between operations  1.51 us (5%)
    pallas_call x1, Pallas kernels, filtered(): pl.pallas_call(functools.partial(filter_kernel, rows, cols, span), in_spe...  6.53 us
    ppermute x1, starting transfers between devices, outer_partner(): lax.ppermute(x, axis, [(i, (i - 1 ^ 1) + 1) for i in range(1, n - 1)])  6.38 us
    ppermute x2, starting transfers between devices, partner(): return lax.ppermute(x, axis, [(i, i ^ 1) for i in range(n)])  6.19 us
    ppermute x1, waiting for transfers between devices, handed_on(): return lax.ppermute(x, 'gy', route)  3.84 us
    ppermute x1, starting transfers between devices, handed_on(): return lax.ppermute(x, 'gy', route)  3.11 us
    ppermute x1, waiting for transfers between devices, outer_partner(): lax.ppermute(x, axis, [(i, (i - 1 ^ 1) + 1) for i in range(1, n - 1)])  2.2 us
    ppermute x2, waiting for transfers between devices, partner(): return lax.ppermute(x, axis, [(i, i ^ 1) for i in range(n)])  1.5 us
    pallas_call x1, Pallas kernels, own_gram(): pl.pallas_call(gram_kernel, in_specs=[vmem()] * 2, out_specs=[vmem()] * 2...  0.86 us
  transfers between devices with their start and end apart: 4, of which 3 were waited for; matrix products, arithmetic and copies ran while one was open for 0% of the time, Pallas kernels for 0%

profile of v5, /device:TPU:49, one launch (start us, length us, event | category | flops | bytes accessed | tf_op | source)
XLA Modules:
  0.0 32.3 jit_solution(10082872030097780120)
XLA Ops:
  0.0 0.0 copy-start
  1.5 0.0 copy-start.1
  1.5 0.1 copy-done
  1.6 0.9 %own_gram.1 = (f32[200,128]{1,0:T(8,128)S(1)}, bf16[200,128]{1,0:T(8,128)(2,1)S(1)}) custom-call(f32[8,128]{1,0:T(8,128)S(1)} %meta_tile.1.meta_ref, bf16[4096,200]{1,0:T(8,128)(2,1)S(1)} %bitcast.3), custom_call_target="tpu_custom_call" | custom-call | flops 327680000 | bytes 1638400 | tf_op jit(solution)/shard_map/own_gram/pallas_call | solution.py:76
  2.5 6.1 %collective-permute-start = (bf16[200,128]{1,0:T(8,128)(2,1)S(1)}, bf16[200,128]{1,0:T(8,128)(2,1)S(1)}, u32[]{:S(2)}, u32[]{:S(2)}) collective-permute-start(bf16[200,128]{1,0:T(8,128)(2,1)S(1)} %get-tuple-element.10.mine_ref), channel_id=1, source_target_pairs={{0,1},{1,0},{2,3},{3,2},{4,5},{5,4},{6,7},{7,6},{8,9},{9,8},{10,11... | collective-permute-start | bytes 153608 | tf_op jit(solution)/shard_map/ppermute | solution.py:339
  8.6 1.5 %collective-permute-done.near_ref = bf16[200,128]{1,0:T(8,128)(2,1)S(1)} collective-permute-done((bf16[200,128]{1,0:T(8,128)(2,1)S(1)}, bf16[200,128]{1,0:T(8,128)(2,1)S(1)}, u32[]{:S(2)}, u32[]{:S(2)}) %collective-permute-start) | collective-permute-done | bytes 51232 | tf_op jit(solution)/shard_map/ppermute | solution.py:339
  10.1 3.1 %collective-permute-start.1 = (bf16[200,128]{1,0:T(8,128)(2,1)S(1)}, bf16[200,128]{1,0:T(8,128)(2,1)S(1)}, u32[]{:S(2)}, u32[]{:S(2)}) collective-permute-start(bf16[200,128]{1,0:T(8,128)(2,1)S(1)} %collective-permute-done.near_ref), channel_id=1, source_target_pairs={{0,2},{2,4},{4,6},{6,8},{8,10},{10,12},{12,14},{14,16},{16,18},{18... | collective-permute-start | bytes 153608 | tf_op jit(solution)/shard_map/ppermute | solution.py:350
  13.2 3.8 %collective-permute-done.1.far_ref = bf16[200,128]{1,0:T(8,128)(2,1)S(1)} collective-permute-done((bf16[200,128]{1,0:T(8,128)(2,1)S(1)}, bf16[200,128]{1,0:T(8,128)(2,1)S(1)}, u32[]{:S(2)}, u32[]{:S(2)}) %collective-permute-start.1) | collective-permute-done | bytes 51232 | tf_op jit(solution)/shard_map/ppermute | solution.py:350
  17.1 6.4 %collective-permute-start.3 = (bf16[2,200,128]{2,1,0:T(8,128)(2,1)S(1)}, bf16[2,200,128]{2,1,0:T(8,128)(2,1)S(1)}, u32[]{:S(2)}, u32[]{:S(2)}) collective-permute-start(bf16[2,200,128]{2,1,0:T(8,128)(2,1)S(1)} %get-tuple-element.12), channel_id=1, source_target_pairs={{32,64},{64,32},{96,128},{128,96},{160,192},{192,160},{33,65},{65,... | collective-permute-start | bytes 307208 | tf_op jit(solution)/shard_map/ppermute | solution.py:344
  23.4 0.1 collective-permute-start.2
  23.5 0.0 copy-done.1
  23.6 2.2 %collective-permute-done.3.far_ref = bf16[2,200,128]{2,1,0:T(8,128)(2,1)S(1)} collective-permute-done((bf16[2,200,128]{2,1,0:T(8,128)(2,1)S(1)}, bf16[2,200,128]{2,1,0:T(8,128)(2,1)S(1)}, u32[]{:S(2)}, u32[]{:S(2)}) %collective-permute-start.3) | collective-permute-done | bytes 102432 | tf_op jit(solution)/shard_map/ppermute | solution.py:344
  25.8 0.0 collective-permute-done.2.near_ref
  25.8 6.5 %filtered.1 = bf16[4096,200]{1,0:T(8,128)(2,1)} custom-call(f32[2,200,128]{2,1,0:T(8,128)S(1)} %get-tuple-element.11.sums_ref, bf16[2,200,128]{2,1,0:T(8,128)(2,1)S(1)} %collective-permute-done.2.near_ref, bf16[2,200,128]{2,1,0:T(8,128)(2,1)S(1)} %collective-permute-done.3.far_ref, f32[32,256]{1,0:T(8,128)S(1)} %pad.4.start_ref, bf16[4096,200]{1,0:T(8,128)(2,1)S(1)} %bitcast.4), custom_call_target="tpu_custom_call" | custom-call | flops 838860800 | bytes 3276800 | tf_op jit(solution)/shard_map/filtered/pallas_call | solution.py:317
  (3 shorter events, 0.0 us)
Async XLA Ops:
  0.0 1.6 %copy-start = (bf16[16,16,16,200]{3,2,1,0:T(8,128)(2,1)S(1)}, bf16[16,16,16,200]{3,2,1,0:T(8,128)(2,1)}, u32[]{:S(2)}) copy-start(bf16[16,16,16,200]{3,2,1,0:T(8,128)(2,1)} %param.4) | copy-start | bytes 4915204
  1.5 22.1 %copy-start.1 = (f32[200,32]{0,1:T(8,128)S(1)}, f32[200,32]{0,1:T(8,128)}, u32[]{:S(2)}) copy-start(f32[200,32]{0,1:T(8,128)} %param.5) | copy-start | bytes 76804
  2.5 7.6 %collective-permute-start = (bf16[200,128]{1,0:T(8,128)(2,1)S(1)}, bf16[200,128]{1,0:T(8,128)(2,1)S(1)}, u32[]{:S(2)}, u32[]{:S(2)}) collective-permute-start(bf16[200,128]{1,0:T(8,128)(2,1)S(1)} %get-tuple-element.10.mine_ref), channel_id=1, source_target_pairs={{0,1},{1,0},{2,3},{3,2},{4,5},{5,4},{6,7},{7,6},{8,9},{9,8},{10,11... | collective-permute-start | bytes 153608 | tf_op jit(solution)/shard_map/ppermute | solution.py:339
  10.1 7.0 %collective-permute-start.1 = (bf16[200,128]{1,0:T(8,128)(2,1)S(1)}, bf16[200,128]{1,0:T(8,128)(2,1)S(1)}, u32[]{:S(2)}, u32[]{:S(2)}) collective-permute-start(bf16[200,128]{1,0:T(8,128)(2,1)S(1)} %collective-permute-done.near_ref), channel_id=1, source_target_pairs={{0,2},{2,4},{4,6},{6,8},{8,10},{10,12},{12,14},{14,16},{16,18},{18... | collective-permute-start | bytes 153608 | tf_op jit(solution)/shard_map/ppermute | solution.py:350
  17.1 8.7 %collective-permute-start.3 = (bf16[2,200,128]{2,1,0:T(8,128)(2,1)S(1)}, bf16[2,200,128]{2,1,0:T(8,128)(2,1)S(1)}, u32[]{:S(2)}, u32[]{:S(2)}) collective-permute-start(bf16[2,200,128]{2,1,0:T(8,128)(2,1)S(1)} %get-tuple-element.12), channel_id=1, source_target_pairs={{32,64},{64,32},{96,128},{128,96},{160,192},{192,160},{33,65},{65,... | collective-permute-start | bytes 307208 | tf_op jit(solution)/shard_map/ppermute | solution.py:344
  23.4 2.3 %collective-permute-start.2 = (bf16[2,200,128]{2,1,0:T(8,128)(2,1)S(1)}, bf16[2,200,128]{2,1,0:T(8,128)(2,1)S(1)}, u32[]{:S(2)}, u32[]{:S(2)}) collective-permute-start(bf16[2,200,128]{2,1,0:T(8,128)(2,1)S(1)} %get-tuple-element.12), channel_id=1, source_target_pairs={{0,32},{32,0},{64,96},{96,64},{128,160},{160,128},{192,224},{224,1... | collective-permute-start | bytes 307208 | tf_op jit(solution)/shard_map/ppermute | solution.py:339
